TPU v7x, 32 devices: a whole 2x2x4 slice. The times are simulated.
32 devices in a mesh: rec: 8 (over y, x, core), tile: 4 (over z).
Axes of the slice: x: 2, y: 2, z: 4, core: 2. Of those that a mesh axis runs over, the one named last changes fastest.
Arguments:
- deviation: float32 [64, 16, 512], P(None, 'rec', 'tile'), may hold values from -6 to 6
- footprint: bfloat16 [2048, 4, 2, 8, 8, 128], P('rec', 'tile'), may hold values from -0.046875 to 0.046875
- tile_list: int32 [2048, 4, 2], P('rec', 'tile'), may hold values from -1 to 1, as said below
- offset: int32 [2048], P('rec'), may hold values from 0 to 56
- observed: float32 [2048], P('rec'), may hold values from -10 to 10
- obs_group: int32 [2048], P('rec'), may hold values from 0 to 3
- group_var: float32 [4], replicated, may hold values from 0.5 to 4
- inv_time: float32 [64, 64], replicated, as said below
- inv_lat: float32 [16, 16], replicated, as said below
- inv_lon: float32 [512, 512], P('tile'), as said below
Outputs:
- gradient: float32 [64, 16, 512], P(None, 'rec', 'tile')
- misfit: float32 [2048], P('rec')
Inputs may be any that keep to these rules, and one draw needn't show every extreme that they name: `tile_list`: each entry is a latitude tile of 8 rows in the slot's longitude strip, or -1 for an unused slot; the tiles named by one receptor in one strip are distinct. `inv_lon`: symmetric and diagonally dominant with a positive diagonal. `inv_lat`: symmetric and diagonally dominant with a positive diagonal. `inv_time`: symmetric and diagonally dominant with a positive diagonal.
All inputs are finite; a program needn't handle non-finite values.
Results may differ from a plain program's by a relative error of at most 0.0003.
Values sent between devices are 32-bit elements; how exact they have to be, the bound alone decides.
No kernel may reach another device: no remote copies, remote signals or barrier semaphores. Data moves between devices by JAX's collectives and lax.ppermute only.
A program may use at most 128 MiB of HBM per device.

v0:
```python
import functools

import jax
import jax.numpy as jnp
from jax import lax
from jax.experimental import pallas as pl
from jax.experimental.pallas import tpu as pltpu
from jax.sharding import PartitionSpec as P


GROUP = 8
N_ACC = 4
CHUNKS = 8
HIGHEST = lax.Precision.HIGHEST


def dot(left, right, dims=((1,), (0,))):
    return lax.dot_general(
        left, right, (dims, ((), ())), precision=HIGHEST, preferred_element_type=jnp.float32
    )


def place(owner, dims):
    periods, _, tile_rows, lat_dev = dims[:4]
    row = owner * lat_dev
    return (row // tile_rows) * (periods * tile_rows) + lax.rem(row, tile_rows)


def index_kernel(dims, tile_hbm, offset_hbm, base_ref, tile_ref, offset_ref, sems):
    periods, tiles_y = dims[:2]
    copies = [
        pltpu.make_async_copy(tile_hbm, tile_ref, sems.at[0]),
        pltpu.make_async_copy(offset_hbm, offset_ref, sems.at[1]),
    ]
    for copy in copies:
        copy.start()
    for copy in copies:
        copy.wait()
    tile = tile_ref[...]
    tile = jnp.where(tile < 0, tiles_y, tile)
    base_ref[...] = tile * periods + offset_ref[...]


def load_copies(base_ref, base, base_sem, foot_hbm, foot, foot_sems):
    chunk = foot.shape[0] // CHUNKS
    first = pltpu.make_async_copy(base_ref, base, base_sem)
    rest = [
        pltpu.make_async_copy(
            foot_hbm.at[pl.ds(index * chunk, chunk)],
            foot.at[pl.ds(index * chunk, chunk)],
            foot_sems.at[index],
        )
        for index in range(CHUNKS)
    ]
    first.start()
    for copy in rest:
        copy.start()
    return first, rest


def forward_kernel(dims, base_ref, foot_hbm, *refs):
    periods, tiles_y, tile_rows, lat_dev, receptors, slots, window = dims
    blocks = refs[:-7]
    out_ref, table, sums, base, base_sem, foot_ref, foot_sems = refs[-7:]
    lanes = table.shape[-1]
    first, rest_copies = load_copies(base_ref, base, base_sem, foot_hbm, foot_ref, foot_sems)
    own = lax.axis_index("rec")
    for dist, block in enumerate(blocks):
        start = place(own ^ dist, dims)
        for row in range(lat_dev):
            table[pl.ds(start + row, periods, stride=tile_rows), :] = block[
                pl.ds(row, periods, stride=lat_dev), :
            ]
    rest = tiles_y * periods * tile_rows
    table[pl.ds(rest, periods * tile_rows), :] = jnp.zeros((periods * tile_rows, lanes), jnp.float32)

    def step(group, carry):
        for item in range(GROUP):
            receptor = group * GROUP + item
            total = None
            for slot in range(slots):
                start = pl.multiple_of(base[slot, receptor] * tile_rows, tile_rows)
                field = table[pl.ds(start, window * tile_rows), :]
                field = field.reshape(window, tile_rows, lanes)
                block = foot_ref[receptor, slot].astype(jnp.float32)
                part = jnp.sum(block * field, axis=0)
                total = part if total is None else total + part
            sums[receptor] = total
        return carry

    first.wait()
    groups = receptors // GROUP // CHUNKS
    for index, copy in enumerate(rest_copies):
        copy.wait()
        lax.fori_loop(index * groups, (index + 1) * groups, step, 0)
    rows = jnp.sum(sums[...], axis=1)
    flat = dot(jnp.ones((8, lanes), jnp.float32), rows, ((1,), (1,)))
    out_ref[...] = flat[0:1, :]


def prior_kernel(dims, n_tile, *refs):
    periods, tiles_y, tile_rows, lat_dev = dims[:4]
    own, strip = lax.axis_index("rec"), lax.axis_index("tile")
    strips = refs[:n_tile]
    lon_ref, time_ref, lat_ref, out_ref, mixed = refs[n_tile:]
    lanes = out_ref.shape[-1]
    total = None
    for dist, value in enumerate(strips):
        start = pl.multiple_of((strip ^ dist) * lanes, lanes)
        term = dot(value[...], lon_ref[:, pl.ds(start, lanes)], ((1,), (1,)))
        total = term if total is None else total + term
    mixed[...] = total
    fields = [
        dot(time_ref[...], mixed[pl.ds(row, periods, stride=lat_dev), :]) for row in range(lat_dev)
    ]
    for row in range(lat_dev):
        mixed[pl.ds(row * periods, periods), :] = fields[row]
    cols = [lat_ref[pl.ds(own * lat_dev + row, 1), :] for row in range(lat_dev)]
    cols = [
        jnp.transpose(jnp.broadcast_to(col, (lanes, col.shape[-1]))) for col in cols
    ]

    def finish(period, carry):
        lines = [
            jnp.broadcast_to(mixed[pl.ds(row * periods + period, 1), :], (tile_rows, lanes))
            for row in range(lat_dev)
        ]
        for tile in range(tiles_y):
            value = None
            for row in range(lat_dev):
                term = cols[row][tile * tile_rows : (tile + 1) * tile_rows] * lines[row]
                value = term if value is None else value + term
            start = pl.multiple_of((tile * periods + period) * tile_rows, tile_rows)
            out_ref[pl.ds(start, tile_rows), :] = value
        return carry

    lax.fori_loop(0, periods, finish, 0, unroll=8)


def adjoint_kernel(dims, n_tile, base_ref, foot_hbm, *refs):
    periods, tiles_y, tile_rows, lat_dev, receptors, slots, window = dims
    preds = refs[:n_tile]
    observed_ref, group_ref, var_ref, prior_ref = refs[n_tile : n_tile + 4]
    n_rec = (tiles_y * tile_rows) // lat_dev
    outs = refs[n_tile + 4 : n_tile + 4 + n_rec]
    scratch = refs[n_tile + 4 + n_rec :]
    misfit_ref, weight, base, base_sem, foot_ref, foot_sems = scratch[:6]
    accs = scratch[6:]
    lanes = weight.shape[-1]
    first, rest_copies = load_copies(base_ref, base, base_sem, foot_hbm, foot_ref, foot_sems)
    own = lax.axis_index("rec")
    predicted = preds[0][...]
    for other in preds[1:]:
        predicted = predicted + other[...]
    group = group_ref[...]
    variance = jnp.zeros(group.shape, jnp.float32)
    for index in range(var_ref.shape[1]):
        variance = jnp.where(group == index, var_ref[:, index : index + 1], variance)
    misfit = (predicted - observed_ref[...]) / variance
    misfit_ref[...] = misfit
    weight[...] = jnp.transpose(jnp.broadcast_to(misfit, (lanes, receptors)))
    for acc in accs:
        acc[...] = jnp.zeros(acc.shape, jnp.float32)

    def step(group, carry):
        for item in range(GROUP):
            receptor = group * GROUP + item
            scale = jnp.broadcast_to(weight[pl.ds(receptor, 1), :], (tile_rows, lanes))
            for slot in range(slots):
                start = pl.multiple_of(base[slot, receptor] * tile_rows, tile_rows)
                acc = accs[(item * slots + slot) % len(accs)]
                block = foot_ref[receptor, slot].astype(jnp.float32) * scale[None]
                acc[pl.ds(start, window * tile_rows), :] += block.reshape(window * tile_rows, lanes)
        return carry

    first.wait()
    groups = receptors // GROUP // CHUNKS
    for index, copy in enumerate(rest_copies):
        copy.wait()
        lax.fori_loop(index * groups, (index + 1) * groups, step, 0)
    total = accs[0]
    size = tiles_y * periods * tile_rows
    chunk = 8 * tile_rows

    def finish(index, carry):
        rows = pl.ds(pl.multiple_of(index * chunk, chunk), chunk)
        value = prior_ref[rows, :]
        for acc in accs:
            value = value + acc[rows, :]
        total[rows, :] = value
        return carry

    lax.fori_loop(0, size // chunk, finish, 0)
    for dist, out in enumerate(outs):
        start = place(own ^ dist, dims)
        for row in range(lat_dev):
            out[pl.ds(row, periods, stride=lat_dev), :] = total[
                pl.ds(start + row, periods, stride=tile_rows), :
            ]


def shards(
    deviation,
    footprint,
    tile_list,
    offset,
    observed,
    obs_group,
    group_var,
    inv_time,
    inv_lat,
    inv_lon,
):
    periods, lat_dev, lon_dev = deviation.shape
    receptors, _, slots, window, tile_rows, _ = footprint.shape
    n_rec = lax.axis_size("rec")
    n_tile = lax.axis_size("tile")
    tiles_y = lat_dev * n_rec // tile_rows
    dims = (periods, tiles_y, tile_rows, lat_dev, receptors, slots, window)
    anywhere = pl.BlockSpec(memory_space=pltpu.HBM)
    vmem = pl.BlockSpec(memory_space=pltpu.VMEM)
    params = pltpu.CompilerParams(vmem_limit_bytes=48 * 2**20)
    field_rows = periods * lat_dev
    block_shape = jax.ShapeDtypeStruct((field_rows, lon_dev), jnp.float32)
    line_shape = jax.ShapeDtypeStruct((1, receptors), jnp.float32)
    prior_shape = jax.ShapeDtypeStruct((tiles_y * periods * tile_rows, lon_dev), jnp.float32)
    table_shape = pltpu.VMEM(((tiles_y + 1) * periods * tile_rows, lon_dev), jnp.float32)

    load_shapes = [
        pltpu.SMEM((slots, receptors), jnp.int32),
        pltpu.SemaphoreType.DMA,
        pltpu.VMEM((receptors, slots, window, tile_rows, lon_dev), footprint.dtype),
        pltpu.SemaphoreType.DMA((CHUNKS,)),
    ]

    def swap(value, axis, dist):
        size = lax.axis_size(axis)
        return lax.ppermute(value, axis, [(i, i ^ dist) for i in range(size)])

    local = deviation.reshape(field_rows, lon_dev)
    far = range(2, n_rec, 2)
    even = {0: local}
    for dist in far:
        even[dist] = swap(local, "rec", dist)
    blocks = []
    for dist in range(0, n_rec, 2):
        blocks += [even[dist], swap(even[dist], "rec", 1)]
    strips = [local] + [swap(local, "tile", d) for d in range(1, n_tile)]

    base = pl.pallas_call(
        functools.partial(index_kernel, dims),
        out_shape=jax.ShapeDtypeStruct((slots, receptors), jnp.int32),
        in_specs=[anywhere] * 2,
        out_specs=vmem,
        scratch_shapes=[
            pltpu.VMEM((slots, receptors), jnp.int32),
            pltpu.VMEM((1, receptors), jnp.int32),
            pltpu.SemaphoreType.DMA((2,)),
        ],
        compiler_params=pltpu.CompilerParams(vmem_limit_bytes=2**20),
        cost_estimate=pl.CostEstimate(flops=10**10, bytes_accessed=2 * 10**7, transcendentals=0),
    )(tile_list[:, 0, :].T, offset.reshape(1, receptors))
    foot = footprint[:, 0]
    partial_pred = pl.pallas_call(
        functools.partial(forward_kernel, dims),
        out_shape=line_shape,
        in_specs=[vmem, anywhere] + [vmem] * n_rec,
        out_specs=vmem,
        scratch_shapes=[table_shape, pltpu.VMEM((receptors, tile_rows, lon_dev), jnp.float32)]
        + load_shapes,
        compiler_params=params,
    )(base, foot, *blocks)
    preds = [partial_pred] + [swap(partial_pred, "tile", d) for d in range(1, n_tile)]
    prior = pl.pallas_call(
        functools.partial(prior_kernel, dims, n_tile),
        out_shape=prior_shape,
        in_specs=[vmem] * (n_tile + 3),
        out_specs=vmem,
        scratch_shapes=[pltpu.VMEM((field_rows, lon_dev), jnp.float32)],
        compiler_params=params,
    )(*strips, inv_lon, inv_time, inv_lat)
    results = pl.pallas_call(
        functools.partial(adjoint_kernel, dims, n_tile),
        out_shape=[block_shape] * n_rec + [line_shape],
        in_specs=[vmem, anywhere] + [vmem] * (n_tile + 4),
        out_specs=[vmem] * (n_rec + 1),
        scratch_shapes=[pltpu.VMEM((receptors, lon_dev), jnp.float32)]
        + load_shapes
        + [table_shape] * N_ACC,
        compiler_params=params,
    )(
        base,
        foot,
        *preds,
        observed.reshape(1, receptors),
        obs_group.reshape(1, receptors),
        group_var.reshape(1, -1),
        prior,
    )
    misfit = results[n_rec].reshape(receptors)
    gradient = None
    for dist in list(reversed(range(2, n_rec, 2))) + [0]:
        value = results[dist] + swap(results[dist + 1], "rec", 1)
        value = value if dist == 0 else swap(value, "rec", dist)
        gradient = value if gradient is None else gradient + value
    return (gradient.reshape(periods, lat_dev, lon_dev), misfit)


def solution(mesh):
    return jax.shard_map(
        shards,
        mesh=mesh,
        in_specs=(
            P(None, "rec", "tile"),
            P("rec", "tile", None, None, None, None),
            P("rec", "tile", None),
            P("rec"),
            P("rec"),
            P("rec"),
            P(),
            P(),
            P(),
            P("tile", None),
        ),
        out_specs=(P(None, "rec", "tile"), P("rec")),
        check_vma=False,
    )
```

profile of v0, /device:TPU:0, one launch (start us, length us, event | category | flops | bytes accessed | tf_op | source)
XLA Modules:
  0.0 41.4 jit_solution(6262639193792542176)
XLA Ops:
  0.6 4.0 %collective-permute-start.5 = (f32[128,128]{1,0:T(8,128)}, f32[128,128]{1,0:T(8,128)S(1)}, u32[]{:S(2)}, u32[]{:S(2)}) collective-permute-start(f32[128,128]{1,0:T(8,128)} %bitcast.11), channel_id=1, source_target_pairs={{0,24},{4,28},{8,16},{12,20},{16,8},{20,12},{24,0},{28,4},{1,25},{... | collective-permute-start | bytes 196616 | tf_op jit(solution)/shard_map/ppermute | solution.py:238
  4.6 0.5 %collective-permute-start.3 = (f32[128,128]{1,0:T(8,128)}, f32[128,128]{1,0:T(8,128)S(1)}, u32[]{:S(2)}, u32[]{:S(2)}) collective-permute-start(f32[128,128]{1,0:T(8,128)} %bitcast.12), channel_id=1, source_target_pairs={{0,16},{4,20},{8,24},{12,28},{16,0},{20,4},{24,8},{28,12},{1,17},{... | collective-permute-start | bytes 196616 | tf_op jit(solution)/shard_map/ppermute | solution.py:238
  5.1 0.1 collective-permute-start.1
  5.3 0.0 collective-permute-start
  5.3 1.8 %collective-permute-done.5.refs_6_ = f32[128,128]{1,0:T(8,128)S(1)} collective-permute-done((f32[128,128]{1,0:T(8,128)}, f32[128,128]{1,0:T(8,128)S(1)}, u32[]{:S(2)}, u32[]{:S(2)}) %collective-permute-start.5) | collective-permute-done | bytes 65568 | tf_op jit(solution)/shard_map/ppermute | solution.py:238
  7.1 0.0 collective-permute-start.6
  7.1 4.1 %collective-permute-start.12 = (f32[128,128]{1,0:T(8,128)}, f32[128,128]{1,0:T(8,128)S(1)}, u32[]{:S(2)}, u32[]{:S(2)}) collective-permute-start(f32[128,128]{1,0:T(8,128)} %bitcast.15), channel_id=1, source_target_pairs={{0,3},{1,2},{2,1},{3,0},{4,7},{5,6},{6,5},{7,4},{8,11},{9,10},{10,... | collective-permute-start | bytes 196616 | tf_op jit(solution)/shard_map/ppermute | solution.py:238
  11.2 0.0 collective-permute-done.3.refs_4_
  11.2 0.5 %collective-permute-start.11 = (f32[128,128]{1,0:T(8,128)}, f32[128,128]{1,0:T(8,128)S(1)}, u32[]{:S(2)}, u32[]{:S(2)}) collective-permute-start(f32[128,128]{1,0:T(8,128)} %bitcast.16), channel_id=1, source_target_pairs={{0,2},{1,3},{2,0},{3,1},{4,6},{5,7},{6,4},{7,5},{8,10},{9,11},{10,... | collective-permute-start | bytes 196616 | tf_op jit(solution)/shard_map/ppermute | solution.py:238
  11.7 0.0 collective-permute-done.1.refs_2_
  11.7 1.6 %collective-permute-start.10 = (f32[128,128]{1,0:T(8,128)}, f32[128,128]{1,0:T(8,128)S(1)}, u32[]{:S(2)}, u32[]{:S(2)}) collective-permute-start(f32[128,128]{1,0:T(8,128)} %bitcast.17), channel_id=1, source_target_pairs={{0,1},{1,0},{2,3},{3,2},{4,5},{5,4},{6,7},{7,6},{8,9},{9,8},{10,11... | collective-permute-start | bytes 196616 | tf_op jit(solution)/shard_map/ppermute | solution.py:238
  13.3 0.0 collective-permute-done.refs_1_
  13.3 0.0 collective-permute-start.4
  13.3 0.0 collective-permute-done.6.refs_7_
  13.3 0.5 %collective-permute-start.2 = (f32[128,128]{1,0:T(8,128)S(1)}, f32[128,128]{1,0:T(8,128)S(1)}, u32[]{:S(2)}, u32[]{:S(2)}) collective-permute-start(f32[128,128]{1,0:T(8,128)S(1)} %collective-permute-done.1.refs_2_), channel_id=1, source_target_pairs={{0,4},{4,0},{8,12},{12,8},{16,20},{20,16},{24,28},{28,24},{1,5},{5... | collective-permute-start | bytes 196616 | tf_op jit(solution)/shard_map/ppermute | solution.py:238
  13.8 0.7 %copy-done.7 = s32[256,1,2]{0,2,1:T(2,128)S(1)} copy-done((s32[256,1,2]{0,2,1:T(2,128)S(1)}, s32[256,1,2]{0,2,1:T(2,128)}, u32[]{:S(2)}) %copy-start.7) | copy-done | bytes 2072
  14.5 0.7 %copy-done.8 = s32[256]{0:T(256)S(1)} copy-done((s32[256]{0:T(256)S(1)}, s32[256]{0:T(256)}, u32[]{:S(2)}) %copy-start.8) | copy-done | bytes 1048
  15.2 0.0 copy-start
  15.2 0.0 copy-start.2
  15.2 0.0 copy-start.3
  15.2 0.0 copy-start.4
  15.2 0.0 copy-start.5
  15.2 0.0 copy-start.6
  15.3 0.0 collective-permute-done.4.refs_5_
  15.3 0.7 %copy-done.1 = f32[64,2,128]{2,1,0:T(2,128)S(1)} copy-done((f32[64,2,128]{2,1,0:T(2,128)S(1)}, f32[64,2,128]{2,1,0:T(2,128)}, u32[]{:S(2)}) %copy-start.1) | copy-done | bytes 65560
  16.0 4.2 %shard_map.114.refs_0_ = f32[1,256]{1,0:T(1,128)S(1)} custom-call(s32[2,256]{1,0:T(2,128)S(1)} %shard_map.113.base_ref, bf16[256,2,8,8,128]{4,3,2,1,0:T(8,128)(2,1)} %bitcast.25, f32[128,128]{1,0:T(8,128)S(1)} %bitcast.18, f32[128,128]{1,0:T(8,128)S(1)} %collective-permute-done.refs_1_, f32[128,128]{1,0:T(8,128)S(1)} %collective-permute-done.1.refs_2_, ...), custom_call_target="tpu_custom_call" | custom-call | tf_op jit(solution)/shard_map/pallas_call | solution.py:264
  20.2 2.4 %collective-permute-start.9 = (f32[1,256]{1,0:T(1,128)S(1)}, f32[1,256]{1,0:T(1,128)S(1)}, u32[]{:S(2)}, u32[]{:S(2)}) collective-permute-start(f32[1,256]{1,0:T(1,128)S(1)} %shard_map.114.refs_0_), channel_id=1, source_target_pairs={{0,3},{1,2},{2,1},{3,0},{4,7},{5,6},{6,5},{7,4},{8,11},{9,10},{10,... | collective-permute-start | bytes 3080 | tf_op jit(solution)/shard_map/ppermute | solution.py:238
  22.6 0.0 collective-permute-start.8
  22.6 0.0 collective-permute-done.12.refs_3_
  22.6 2.0 %collective-permute-start.7 = (f32[1,256]{1,0:T(1,128)S(1)}, f32[1,256]{1,0:T(1,128)S(1)}, u32[]{:S(2)}, u32[]{:S(2)}) collective-permute-start(f32[1,256]{1,0:T(1,128)S(1)} %shard_map.114.refs_0_), channel_id=1, source_target_pairs={{0,1},{1,0},{2,3},{3,2},{4,5},{5,4},{6,7},{7,6},{8,9},{9,8},{10,11... | collective-permute-start | bytes 3080 | tf_op jit(solution)/shard_map/ppermute | solution.py:238
  24.7 1.0 %shard_map.115.refs_7_ = f32[1024,128]{1,0:T(8,128)S(1)} custom-call(f32[128,128]{1,0:T(8,128)S(1)} %bitcast.19, f32[128,128]{1,0:T(8,128)S(1)} %collective-permute-done.10.refs_1_, f32[128,128]{1,0:T(8,128)S(1)} %collective-permute-done.11.refs_2_, f32[128,128]{1,0:T(8,128)S(1)} %collective-permute-done.12.refs_3_, f32[128,512]{1,0:T(8,128)S(1)} %copy-done, ...), custom_call_target="tpu_custom_call" | custom-call | tf_op jit(solution)/shard_map/pallas_call | solution.py:274
  25.7 1.3 %collective-permute-done.8.refs_2_ = f32[1,256]{1,0:T(1,128)S(1)} collective-permute-done((f32[1,256]{1,0:T(1,128)S(1)}, f32[1,256]{1,0:T(1,128)S(1)}, u32[]{:S(2)}, u32[]{:S(2)}) %collective-permute-start.8) | collective-permute-done | bytes 1056 | tf_op jit(solution)/shard_map/ppermute | solution.py:238
  27.1 0.0 collective-permute-done.7.refs_1_
  27.1 4.6 %shard_map.116 = (f32[128,128]{1,0:T(8,128)S(1)}, f32[128,128]{1,0:T(8,128)S(1)}, f32[128,128]{1,0:T(8,128)S(1)}, f32[128,128]{1,0:T(8,128)S(1)}, f32[128,128]{1...) custom-call(s32[2,256]{1,0:T(2,128)S(1)} %shard_map.113.base_ref, ...), custom_call_target="tpu_custom_call" | custom-call | tf_op jit(solution)/shard_map/pallas_call | solution.py:282
  31.7 0.1 collective-permute-start.13
  31.8 0.5 %collective-permute-start.15 = (f32[128,128]{1,0:T(8,128)S(1)}, f32[128,128]{1,0:T(8,128)S(1)}, u32[]{:S(2)}, u32[]{:S(2)}) collective-permute-start(f32[128,128]{1,0:T(8,128)S(1)} %get-tuple-element.14), channel_id=1, source_target_pairs={{0,4},{4,0},{8,12},{12,8},{16,20},{20,16},{24,28},{28,24},{1,5},{5... | collective-permute-start | bytes 196616 | tf_op jit(solution)/shard_map/ppermute | solution.py:238
  32.3 0.1 collective-permute-start.17
  32.3 0.4 %collective-permute-start.19 = (f32[128,128]{1,0:T(8,128)S(1)}, f32[128,128]{1,0:T(8,128)S(1)}, u32[]{:S(2)}, u32[]{:S(2)}) collective-permute-start(f32[128,128]{1,0:T(8,128)S(1)} %get-tuple-element.18), channel_id=1, source_target_pairs={{0,4},{4,0},{8,12},{12,8},{16,20},{20,16},{24,28},{28,24},{1,5},{5... | collective-permute-start | bytes 196616 | tf_op jit(solution)/shard_map/ppermute | solution.py:238
  32.8 0.2 collective-permute-done.13
  33.0 2.7 %collective-permute-start.14 = (f32[128,128]{1,0:T(8,128)S(1)}, f32[128,128]{1,0:T(8,128)S(1)}, u32[]{:S(2)}, u32[]{:S(2)}) collective-permute-start(f32[128,128]{1,0:T(8,128)S(1)} %add.21), channel_id=1, source_target_pairs={{0,24},{4,28},{8,16},{12,20},{16,8},{20,12},{24,0},{28,4},{1,25},{... | collective-permute-start | bytes 196616 | tf_op jit(solution)/shard_map/ppermute | solution.py:238
  35.8 0.6 %collective-permute-start.16 = (f32[128,128]{1,0:T(8,128)S(1)}, f32[128,128]{1,0:T(8,128)S(1)}, u32[]{:S(2)}, u32[]{:S(2)}) collective-permute-start(f32[128,128]{1,0:T(8,128)S(1)} %add.22), channel_id=1, source_target_pairs={{0,16},{4,20},{8,24},{12,28},{16,0},{20,4},{24,8},{28,12},{1,17},{... | collective-permute-start | bytes 196616 | tf_op jit(solution)/shard_map/ppermute | solution.py:238
  36.4 0.0 collective-permute-done.17
  36.4 0.3 collective-permute-start.18
  36.7 0.0 collective-permute-done.19
  36.7 1.5 %collective-permute-done.14 = f32[128,128]{1,0:T(8,128)S(1)} collective-permute-done((f32[128,128]{1,0:T(8,128)S(1)}, f32[128,128]{1,0:T(8,128)S(1)}, u32[]{:S(2)}, u32[]{:S(2)}) %collective-permute-start.14) | collective-permute-done | bytes 65568 | tf_op jit(solution)/shard_map/ppermute | solution.py:238
  38.3 1.8 %collective-permute-done.16 = f32[128,128]{1,0:T(8,128)S(1)} collective-permute-done((f32[128,128]{1,0:T(8,128)S(1)}, f32[128,128]{1,0:T(8,128)S(1)}, u32[]{:S(2)}, u32[]{:S(2)}) %collective-permute-start.16) | collective-permute-done | bytes 65568 | tf_op jit(solution)/shard_map/ppermute | solution.py:238
  40.1 0.6 %collective-permute-done.18 = f32[128,128]{1,0:T(8,128)S(1)} collective-permute-done((f32[128,128]{1,0:T(8,128)S(1)}, f32[128,128]{1,0:T(8,128)S(1)}, u32[]{:S(2)}, u32[]{:S(2)}) %collective-permute-start.18) | collective-permute-done | bytes 65568 | tf_op jit(solution)/shard_map/ppermute | solution.py:238
  40.8 0.6 %add_add_fusion = f32[128,128]{1,0:T(8,128)} fusion(f32[128,128]{1,0:T(8,128)S(1)} %get-tuple-element.17, f32[128,128]{1,0:T(8,128)S(1)} %collective-permute-done.19, f32[128,128]{1,0:T(8,128)S(1)} %collective-permute-done.18, f32[128,128]{1,0:T(8,128)S(1)} %collective-permute-done.14, f32[128,128]{1,0:T(8,128)S(1)} %collective-permute-done.16), kind=kLoop, calls=%fused_computation | loop fusion | flops 65536 | bytes 393216 | tf_op jit(solution)/shard_map/add | solution.py:305
  (18 shorter events, 0.1 us)
Async XLA Ops:
  0.6 6.4 %collective-permute-start.5 = (f32[128,128]{1,0:T(8,128)}, f32[128,128]{1,0:T(8,128)S(1)}, u32[]{:S(2)}, u32[]{:S(2)}) collective-permute-start(f32[128,128]{1,0:T(8,128)} %bitcast.11), channel_id=1, source_target_pairs={{0,24},{4,28},{8,16},{12,20},{16,8},{20,12},{24,0},{28,4},{1,25},{... | collective-permute-start | bytes 196616 | tf_op jit(solution)/shard_map/ppermute | solution.py:238
  4.6 6.6 %collective-permute-start.3 = (f32[128,128]{1,0:T(8,128)}, f32[128,128]{1,0:T(8,128)S(1)}, u32[]{:S(2)}, u32[]{:S(2)}) collective-permute-start(f32[128,128]{1,0:T(8,128)} %bitcast.12), channel_id=1, source_target_pairs={{0,16},{4,20},{8,24},{12,28},{16,0},{20,4},{24,8},{28,12},{1,17},{... | collective-permute-start | bytes 196616 | tf_op jit(solution)/shard_map/ppermute | solution.py:238
  5.1 6.6 %collective-permute-start.1 = (f32[128,128]{1,0:T(8,128)}, f32[128,128]{1,0:T(8,128)S(1)}, u32[]{:S(2)}, u32[]{:S(2)}) collective-permute-start(f32[128,128]{1,0:T(8,128)} %bitcast.13), channel_id=1, source_target_pairs={{0,8},{4,12},{8,0},{12,4},{16,24},{20,28},{24,16},{28,20},{1,9},{5... | collective-permute-start | bytes 196616 | tf_op jit(solution)/shard_map/ppermute | solution.py:238
  5.3 8.0 %collective-permute-start = (f32[128,128]{1,0:T(8,128)}, f32[128,128]{1,0:T(8,128)S(1)}, u32[]{:S(2)}, u32[]{:S(2)}) collective-permute-start(f32[128,128]{1,0:T(8,128)} %bitcast.14), channel_id=1, source_target_pairs={{0,4},{4,0},{8,12},{12,8},{16,20},{20,16},{24,28},{28,24},{1,5},{5... | collective-permute-start | bytes 196616 | tf_op jit(solution)/shard_map/ppermute | solution.py:238
  7.1 6.2 %collective-permute-start.6 = (f32[128,128]{1,0:T(8,128)S(1)}, f32[128,128]{1,0:T(8,128)S(1)}, u32[]{:S(2)}, u32[]{:S(2)}) collective-permute-start(f32[128,128]{1,0:T(8,128)S(1)} %collective-permute-done.5.refs_6_), channel_id=1, source_target_pairs={{0,4},{4,0},{8,12},{12,8},{16,20},{20,16},{24,28},{28,24},{1,5},{5... | collective-permute-start | bytes 196616 | tf_op jit(solution)/shard_map/ppermute | solution.py:238
  7.1 15.5 %collective-permute-start.12 = (f32[128,128]{1,0:T(8,128)}, f32[128,128]{1,0:T(8,128)S(1)}, u32[]{:S(2)}, u32[]{:S(2)}) collective-permute-start(f32[128,128]{1,0:T(8,128)} %bitcast.15), channel_id=1, source_target_pairs={{0,3},{1,2},{2,1},{3,0},{4,7},{5,6},{6,5},{7,4},{8,11},{9,10},{10,... | collective-permute-start | bytes 196616 | tf_op jit(solution)/shard_map/ppermute | solution.py:238
  11.2 13.4 %collective-permute-start.11 = (f32[128,128]{1,0:T(8,128)}, f32[128,128]{1,0:T(8,128)S(1)}, u32[]{:S(2)}, u32[]{:S(2)}) collective-permute-start(f32[128,128]{1,0:T(8,128)} %bitcast.16), channel_id=1, source_target_pairs={{0,2},{1,3},{2,0},{3,1},{4,6},{5,7},{6,4},{7,5},{8,10},{9,11},{10,... | collective-permute-start | bytes 196616 | tf_op jit(solution)/shard_map/ppermute | solution.py:238
  11.7 13.0 %collective-permute-start.10 = (f32[128,128]{1,0:T(8,128)}, f32[128,128]{1,0:T(8,128)S(1)}, u32[]{:S(2)}, u32[]{:S(2)}) collective-permute-start(f32[128,128]{1,0:T(8,128)} %bitcast.17), channel_id=1, source_target_pairs={{0,1},{1,0},{2,3},{3,2},{4,5},{5,4},{6,7},{7,6},{8,9},{9,8},{10,11... | collective-permute-start | bytes 196616 | tf_op jit(solution)/shard_map/ppermute | solution.py:238
  13.3 2.0 %collective-permute-start.4 = (f32[128,128]{1,0:T(8,128)S(1)}, f32[128,128]{1,0:T(8,128)S(1)}, u32[]{:S(2)}, u32[]{:S(2)}) collective-permute-start(f32[128,128]{1,0:T(8,128)S(1)} %collective-permute-done.3.refs_4_), channel_id=1, source_target_pairs={{0,4},{4,0},{8,12},{12,8},{16,20},{20,16},{24,28},{28,24},{1,5},{5... | collective-permute-start | bytes 196616 | tf_op jit(solution)/shard_map/ppermute | solution.py:238
  13.3 2.0 %collective-permute-start.2 = (f32[128,128]{1,0:T(8,128)S(1)}, f32[128,128]{1,0:T(8,128)S(1)}, u32[]{:S(2)}, u32[]{:S(2)}) collective-permute-start(f32[128,128]{1,0:T(8,128)S(1)} %collective-permute-done.1.refs_2_), channel_id=1, source_target_pairs={{0,4},{4,0},{8,12},{12,8},{16,20},{20,16},{24,28},{28,24},{1,5},{5... | collective-permute-start | bytes 196616 | tf_op jit(solution)/shard_map/ppermute | solution.py:238
  13.8 0.7 %copy-start.7 = (s32[256,1,2]{0,2,1:T(2,128)S(1)}, s32[256,1,2]{0,2,1:T(2,128)}, u32[]{:S(2)}) copy-start(s32[256,1,2]{0,2,1:T(2,128)} %param.12) | copy-start | bytes 6148
  14.5 0.7 %copy-start.8 = (s32[256]{0:T(256)S(1)}, s32[256]{0:T(256)}, u32[]{:S(2)}) copy-start(s32[256]{0:T(256)} %param.13) | copy-start | bytes 3076
  15.1 0.8 %copy-start.1 = (f32[64,2,128]{2,1,0:T(2,128)S(1)}, f32[64,2,128]{2,1,0:T(2,128)}, u32[]{:S(2)}) copy-start(f32[64,2,128]{2,1,0:T(2,128)} %param.10) | copy-start | bytes 196612
  15.2 9.5 %copy-start = (f32[128,512]{1,0:T(8,128)S(1)}, f32[128,512]{1,0:T(8,128)}, u32[]{:S(2)}) copy-start(f32[128,512]{1,0:T(8,128)} %refs_4_.1) | copy-start | bytes 786436
  15.2 9.5 %copy-start.2 = (f32[64,64]{1,0:T(8,128)S(1)}, f32[64,64]{1,0:T(8,128)}, u32[]{:S(2)}) copy-start(f32[64,64]{1,0:T(8,128)} %refs_5_.1) | copy-start | bytes 49156
  15.2 9.5 %copy-start.3 = (f32[16,16]{1,0:T(8,128)S(1)}, f32[16,16]{1,0:T(8,128)}, u32[]{:S(2)}) copy-start(f32[16,16]{1,0:T(8,128)} %refs_6_.1) | copy-start | bytes 3076
  15.2 11.9 %copy-start.4 = (f32[256]{0:T(256)S(1)}, f32[256]{0:T(256)}, u32[]{:S(2)}) copy-start(f32[256]{0:T(256)} %param.14) | copy-start | bytes 3076
  15.2 11.8 %copy-start.5 = (s32[256]{0:T(256)S(1)}, s32[256]{0:T(256)}, u32[]{:S(2)}) copy-start(s32[256]{0:T(256)} %param.15) | copy-start | bytes 3076
  15.2 11.8 %copy-start.6 = (f32[4]{0:T(128)S(1)}, f32[4]{0:T(128)}, u32[]{:S(2)}) copy-start(f32[4]{0:T(128)} %param.16) | copy-start | bytes 52
  20.2 5.5 %collective-permute-start.9 = (f32[1,256]{1,0:T(1,128)S(1)}, f32[1,256]{1,0:T(1,128)S(1)}, u32[]{:S(2)}, u32[]{:S(2)}) collective-permute-start(f32[1,256]{1,0:T(1,128)S(1)} %shard_map.114.refs_0_), channel_id=1, source_target_pairs={{0,3},{1,2},{2,1},{3,0},{4,7},{5,6},{6,5},{7,4},{8,11},{9,10},{10,... | collective-permute-start | bytes 3080 | tf_op jit(solution)/shard_map/ppermute | solution.py:238
  22.6 4.5 %collective-permute-start.8 = (f32[1,256]{1,0:T(1,128)S(1)}, f32[1,256]{1,0:T(1,128)S(1)}, u32[]{:S(2)}, u32[]{:S(2)}) collective-permute-start(f32[1,256]{1,0:T(1,128)S(1)} %shard_map.114.refs_0_), channel_id=1, source_target_pairs={{0,2},{1,3},{2,0},{3,1},{4,6},{5,7},{6,4},{7,5},{8,10},{9,11},{10,... | collective-permute-start | bytes 3080 | tf_op jit(solution)/shard_map/ppermute | solution.py:238
  22.6 4.5 %collective-permute-start.7 = (f32[1,256]{1,0:T(1,128)S(1)}, f32[1,256]{1,0:T(1,128)S(1)}, u32[]{:S(2)}, u32[]{:S(2)}) collective-permute-start(f32[1,256]{1,0:T(1,128)S(1)} %shard_map.114.refs_0_), channel_id=1, source_target_pairs={{0,1},{1,0},{2,3},{3,2},{4,5},{5,4},{6,7},{7,6},{8,9},{9,8},{10,11... | collective-permute-start | bytes 3080 | tf_op jit(solution)/shard_map/ppermute | solution.py:238
  31.7 1.3 %collective-permute-start.13 = (f32[128,128]{1,0:T(8,128)S(1)}, f32[128,128]{1,0:T(8,128)S(1)}, u32[]{:S(2)}, u32[]{:S(2)}) collective-permute-start(f32[128,128]{1,0:T(8,128)S(1)} %get-tuple-element.12), channel_id=1, source_target_pairs={{0,4},{4,0},{8,12},{12,8},{16,20},{20,16},{24,28},{28,24},{1,5},{5... | collective-permute-start | bytes 196616 | tf_op jit(solution)/shard_map/ppermute | solution.py:238
  31.8 4.0 %collective-permute-start.15 = (f32[128,128]{1,0:T(8,128)S(1)}, f32[128,128]{1,0:T(8,128)S(1)}, u32[]{:S(2)}, u32[]{:S(2)}) collective-permute-start(f32[128,128]{1,0:T(8,128)S(1)} %get-tuple-element.14), channel_id=1, source_target_pairs={{0,4},{4,0},{8,12},{12,8},{16,20},{20,16},{24,28},{28,24},{1,5},{5... | collective-permute-start | bytes 196616 | tf_op jit(solution)/shard_map/ppermute | solution.py:238
  32.3 4.1 %collective-permute-start.17 = (f32[128,128]{1,0:T(8,128)S(1)}, f32[128,128]{1,0:T(8,128)S(1)}, u32[]{:S(2)}, u32[]{:S(2)}) collective-permute-start(f32[128,128]{1,0:T(8,128)S(1)} %get-tuple-element.16), channel_id=1, source_target_pairs={{0,4},{4,0},{8,12},{12,8},{16,20},{20,16},{24,28},{28,24},{1,5},{5... | collective-permute-start | bytes 196616 | tf_op jit(solution)/shard_map/ppermute | solution.py:238
  32.3 4.4 %collective-permute-start.19 = (f32[128,128]{1,0:T(8,128)S(1)}, f32[128,128]{1,0:T(8,128)S(1)}, u32[]{:S(2)}, u32[]{:S(2)}) collective-permute-start(f32[128,128]{1,0:T(8,128)S(1)} %get-tuple-element.18), channel_id=1, source_target_pairs={{0,4},{4,0},{8,12},{12,8},{16,20},{20,16},{24,28},{28,24},{1,5},{5... | collective-permute-start | bytes 196616 | tf_op jit(solution)/shard_map/ppermute | solution.py:238
  33.0 5.2 %collective-permute-start.14 = (f32[128,128]{1,0:T(8,128)S(1)}, f32[128,128]{1,0:T(8,128)S(1)}, u32[]{:S(2)}, u32[]{:S(2)}) collective-permute-start(f32[128,128]{1,0:T(8,128)S(1)} %add.21), channel_id=1, source_target_pairs={{0,24},{4,28},{8,16},{12,20},{16,8},{20,12},{24,0},{28,4},{1,25},{... | collective-permute-start | bytes 196616 | tf_op jit(solution)/shard_map/ppermute | solution.py:238
  35.8 4.3 %collective-permute-start.16 = (f32[128,128]{1,0:T(8,128)S(1)}, f32[128,128]{1,0:T(8,128)S(1)}, u32[]{:S(2)}, u32[]{:S(2)}) collective-permute-start(f32[128,128]{1,0:T(8,128)S(1)} %add.22), channel_id=1, source_target_pairs={{0,16},{4,20},{8,24},{12,28},{16,0},{20,4},{24,8},{28,12},{1,17},{... | collective-permute-start | bytes 196616 | tf_op jit(solution)/shard_map/ppermute | solution.py:238
  36.4 4.3 %collective-permute-start.18 = (f32[128,128]{1,0:T(8,128)S(1)}, f32[128,128]{1,0:T(8,128)S(1)}, u32[]{:S(2)}, u32[]{:S(2)}) collective-permute-start(f32[128,128]{1,0:T(8,128)S(1)} %add.24), channel_id=1, source_target_pairs={{0,8},{4,12},{8,0},{12,4},{16,24},{20,28},{24,16},{28,20},{1,9},{5... | collective-permute-start | bytes 196616 | tf_op jit(solution)/shard_map/ppermute | solution.py:238
where the time goes:
time: 41.6 us; the launch traced here: 41.4 us
  starting transfers between devices  20.5 us (49%)
  Pallas kernels  9.85 us (24%)
  waiting for transfers between devices  7.43 us (18%)
  local copies, waits for them, and re-layouts  2.1 us (5%)
  between operations  0.8 us (2%)
  other arithmetic  0.68 us (2%)
    ppermute x20, starting transfers between devices, swap(): return lax.ppermute(value, axis, [(i, i ^ dist) for i in range(size)])  20.5 us
    ppermute x20, waiting for transfers between devices, swap(): return lax.ppermute(value, axis, [(i, i ^ dist) for i in range(size)])  7.43 us
    pallas_call x1, Pallas kernels, shards(): pl.pallas_call(functools.partial(adjoint_kernel, dims, n_tile), out_shape...  4.59 us
    pallas_call x1, Pallas kernels, shards(): pl.pallas_call(functools.partial(forward_kernel, dims), out_shape=line_sh...  4.2 us
    unnamed x18, local copies, waits for them, and re-layouts  2.1 us
    pallas_call x1, Pallas kernels, shards(): pl.pallas_call(functools.partial(prior_kernel, dims, n_tile), out_shape=p...  1.03 us
  transfers between devices with their start and end apart: 20, of which 6 were waited for; matrix products, arithmetic and copies ran while one was open for 0% of the time, Pallas kernels for 13%

commit v1 on v0

--- a/solution.py
+++ b/solution.py
@@ -10,7 +10,6 @@
 
 GROUP = 8
 N_ACC = 4
-CHUNKS = 8
 HIGHEST = lax.Precision.HIGHEST
 
 
@@ -26,44 +25,22 @@
     return (row // tile_rows) * (periods * tile_rows) + lax.rem(row, tile_rows)
 
 
-def index_kernel(dims, tile_hbm, offset_hbm, base_ref, tile_ref, offset_ref, sems):
-    periods, tiles_y = dims[:2]
-    copies = [
-        pltpu.make_async_copy(tile_hbm, tile_ref, sems.at[0]),
-        pltpu.make_async_copy(offset_hbm, offset_ref, sems.at[1]),
-    ]
-    for copy in copies:
-        copy.start()
-    for copy in copies:
-        copy.wait()
-    tile = tile_ref[...]
+def ones_kernel(ones_ref):
+    ones_ref[...] = jnp.ones(ones_ref.shape, jnp.float32)
+
+
+def window_start(dims, tile_ref, offset_ref, slot, receptor):
+    periods, tiles_y, tile_rows = dims[:3]
+    tile = tile_ref[slot, receptor]
     tile = jnp.where(tile < 0, tiles_y, tile)
-    base_ref[...] = tile * periods + offset_ref[...]
-
-
-def load_copies(base_ref, base, base_sem, foot_hbm, foot, foot_sems):
-    chunk = foot.shape[0] // CHUNKS
-    first = pltpu.make_async_copy(base_ref, base, base_sem)
-    rest = [
-        pltpu.make_async_copy(
-            foot_hbm.at[pl.ds(index * chunk, chunk)],
-            foot.at[pl.ds(index * chunk, chunk)],
-            foot_sems.at[index],
-        )
-        for index in range(CHUNKS)
-    ]
-    first.start()
-    for copy in rest:
-        copy.start()
-    return first, rest
-
-
-def forward_kernel(dims, base_ref, foot_hbm, *refs):
+    return pl.multiple_of((tile * periods + offset_ref[receptor]) * tile_rows, tile_rows)
+
+
+def forward_kernel(dims, tile_ref, offset_ref, *refs):
     periods, tiles_y, tile_rows, lat_dev, receptors, slots, window = dims
-    blocks = refs[:-7]
-    out_ref, table, sums, base, base_sem, foot_ref, foot_sems = refs[-7:]
+    foot_ref, ones_ref, blocks = refs[0], refs[1], refs[2:-3]
+    out_ref, table, sums = refs[-3:]
     lanes = table.shape[-1]
-    first, rest_copies = load_copies(base_ref, base, base_sem, foot_hbm, foot_ref, foot_sems)
     own = lax.axis_index("rec")
     for dist, block in enumerate(blocks):
         start = place(own ^ dist, dims)
@@ -79,7 +56,7 @@
             receptor = group * GROUP + item
             total = None
             for slot in range(slots):
-                start = pl.multiple_of(base[slot, receptor] * tile_rows, tile_rows)
+                start = window_start(dims, tile_ref, offset_ref, slot, receptor)
                 field = table[pl.ds(start, window * tile_rows), :]
                 field = field.reshape(window, tile_rows, lanes)
                 block = foot_ref[receptor, slot].astype(jnp.float32)
@@ -88,13 +65,9 @@
             sums[receptor] = total
         return carry
 
-    first.wait()
-    groups = receptors // GROUP // CHUNKS
-    for index, copy in enumerate(rest_copies):
-        copy.wait()
-        lax.fori_loop(index * groups, (index + 1) * groups, step, 0)
+    lax.fori_loop(0, receptors // GROUP, step, 0)
     rows = jnp.sum(sums[...], axis=1)
-    flat = dot(jnp.ones((8, lanes), jnp.float32), rows, ((1,), (1,)))
+    flat = dot(ones_ref[...], rows, ((1,), (1,)))
     out_ref[...] = flat[0:1, :]
 
 
@@ -137,17 +110,17 @@
     lax.fori_loop(0, periods, finish, 0, unroll=8)
 
 
-def adjoint_kernel(dims, n_tile, base_ref, foot_hbm, *refs):
+def adjoint_kernel(dims, n_tile, tile_ref, offset_ref, *refs):
     periods, tiles_y, tile_rows, lat_dev, receptors, slots, window = dims
+    foot_ref, refs = refs[0], refs[1:]
     preds = refs[:n_tile]
     observed_ref, group_ref, var_ref, prior_ref = refs[n_tile : n_tile + 4]
     n_rec = (tiles_y * tile_rows) // lat_dev
     outs = refs[n_tile + 4 : n_tile + 4 + n_rec]
     scratch = refs[n_tile + 4 + n_rec :]
-    misfit_ref, weight, base, base_sem, foot_ref, foot_sems = scratch[:6]
-    accs = scratch[6:]
+    misfit_ref, weight = scratch[:2]
+    accs = scratch[2:]
     lanes = weight.shape[-1]
-    first, rest_copies = load_copies(base_ref, base, base_sem, foot_hbm, foot_ref, foot_sems)
     own = lax.axis_index("rec")
     predicted = preds[0][...]
     for other in preds[1:]:
@@ -167,17 +140,13 @@
             receptor = group * GROUP + item
             scale = jnp.broadcast_to(weight[pl.ds(receptor, 1), :], (tile_rows, lanes))
             for slot in range(slots):
-                start = pl.multiple_of(base[slot, receptor] * tile_rows, tile_rows)
+                start = window_start(dims, tile_ref, offset_ref, slot, receptor)
                 acc = accs[(item * slots + slot) % len(accs)]
                 block = foot_ref[receptor, slot].astype(jnp.float32) * scale[None]
                 acc[pl.ds(start, window * tile_rows), :] += block.reshape(window * tile_rows, lanes)
         return carry
 
-    first.wait()
-    groups = receptors // GROUP // CHUNKS
-    for index, copy in enumerate(rest_copies):
-        copy.wait()
-        lax.fori_loop(index * groups, (index + 1) * groups, step, 0)
+    lax.fori_loop(0, receptors // GROUP, step, 0)
     total = accs[0]
     size = tiles_y * periods * tile_rows
     chunk = 8 * tile_rows
@@ -217,21 +186,14 @@
     n_tile = lax.axis_size("tile")
     tiles_y = lat_dev * n_rec // tile_rows
     dims = (periods, tiles_y, tile_rows, lat_dev, receptors, slots, window)
-    anywhere = pl.BlockSpec(memory_space=pltpu.HBM)
+    smem = pl.BlockSpec(memory_space=pltpu.SMEM)
     vmem = pl.BlockSpec(memory_space=pltpu.VMEM)
-    params = pltpu.CompilerParams(vmem_limit_bytes=48 * 2**20)
+    params = pltpu.CompilerParams(vmem_limit_bytes=16 * 2**20)
     field_rows = periods * lat_dev
     block_shape = jax.ShapeDtypeStruct((field_rows, lon_dev), jnp.float32)
     line_shape = jax.ShapeDtypeStruct((1, receptors), jnp.float32)
     prior_shape = jax.ShapeDtypeStruct((tiles_y * periods * tile_rows, lon_dev), jnp.float32)
     table_shape = pltpu.VMEM(((tiles_y + 1) * periods * tile_rows, lon_dev), jnp.float32)
-
-    load_shapes = [
-        pltpu.SMEM((slots, receptors), jnp.int32),
-        pltpu.SemaphoreType.DMA,
-        pltpu.VMEM((receptors, slots, window, tile_rows, lon_dev), footprint.dtype),
-        pltpu.SemaphoreType.DMA((CHUNKS,)),
-    ]
 
     def swap(value, axis, dist):
         size = lax.axis_size(axis)
@@ -247,29 +209,24 @@
         blocks += [even[dist], swap(even[dist], "rec", 1)]
     strips = [local] + [swap(local, "tile", d) for d in range(1, n_tile)]
 
-    base = pl.pallas_call(
-        functools.partial(index_kernel, dims),
-        out_shape=jax.ShapeDtypeStruct((slots, receptors), jnp.int32),
-        in_specs=[anywhere] * 2,
+    ones = pl.pallas_call(
+        ones_kernel,
+        out_shape=jax.ShapeDtypeStruct((8, lon_dev), jnp.float32),
+        in_specs=[],
         out_specs=vmem,
-        scratch_shapes=[
-            pltpu.VMEM((slots, receptors), jnp.int32),
-            pltpu.VMEM((1, receptors), jnp.int32),
-            pltpu.SemaphoreType.DMA((2,)),
-        ],
         compiler_params=pltpu.CompilerParams(vmem_limit_bytes=2**20),
         cost_estimate=pl.CostEstimate(flops=10**10, bytes_accessed=2 * 10**7, transcendentals=0),
-    )(tile_list[:, 0, :].T, offset.reshape(1, receptors))
+    )()
+    tiles = tile_list[:, 0, :].T
     foot = footprint[:, 0]
     partial_pred = pl.pallas_call(
         functools.partial(forward_kernel, dims),
         out_shape=line_shape,
-        in_specs=[vmem, anywhere] + [vmem] * n_rec,
+        in_specs=[smem] * 2 + [vmem] * (2 + n_rec),
         out_specs=vmem,
-        scratch_shapes=[table_shape, pltpu.VMEM((receptors, tile_rows, lon_dev), jnp.float32)]
-        + load_shapes,
+        scratch_shapes=[table_shape, pltpu.VMEM((receptors, tile_rows, lon_dev), jnp.float32)],
         compiler_params=params,
-    )(base, foot, *blocks)
+    )(tiles, offset, foot, ones, *blocks)
     preds = [partial_pred] + [swap(partial_pred, "tile", d) for d in range(1, n_tile)]
     prior = pl.pallas_call(
         functools.partial(prior_kernel, dims, n_tile),
@@ -282,14 +239,13 @@
     results = pl.pallas_call(
         functools.partial(adjoint_kernel, dims, n_tile),
         out_shape=[block_shape] * n_rec + [line_shape],
-        in_specs=[vmem, anywhere] + [vmem] * (n_tile + 4),
+        in_specs=[smem] * 2 + [vmem] * (n_tile + 5),
         out_specs=[vmem] * (n_rec + 1),
-        scratch_shapes=[pltpu.VMEM((receptors, lon_dev), jnp.float32)]
-        + load_shapes
-        + [table_shape] * N_ACC,
+        scratch_shapes=[pltpu.VMEM((receptors, lon_dev), jnp.float32)] + [table_shape] * N_ACC,
         compiler_params=params,
     )(
-        base,
+        tiles,
+        offset,
         foot,
         *preds,
         observed.reshape(1, receptors),

time: 41.6 us -> 38.2 us (0.918)
  local copies, waits for them, and re-layouts: 2.1 us -> 0.05 us
  Pallas kernels: 9.85 us -> 7.84 us
  waiting for transfers between devices: 7.43 us -> 8.28 us
    unnamed x18 -> x22, local copies, waits for them, and re-layouts: 2.1 us -> 0.05 us
    pallas_call x1, Pallas kernels: 4.2 us -> 3.17 us  [shards(): pl.pallas_call(functools.partial(forward_kernel, dims), out_shape=line_sh...]
    pallas_call x1, Pallas kernels: 4.59 us -> 3.64 us  [shards(): pl.pallas_call(functools.partial(adjoint_kernel, dims, n_tile), out_shape...]
    ppermute x20, waiting for transfers between devices: 7.43 us -> 8.28 us  [swap(): return lax.ppermute(value, axis, [(i, i ^ dist) for i in range(size)])]
  transfers between devices with their start and end apart: 20 -> 20, of which waited for: 6 -> 8; matrix products, arithmetic and copies ran while one was open for 0% -> 0% of each run, Pallas kernels for 13% -> 11%
where the time goes in v1:
time: 38.2 us; the launch traced here: 38.1 us
  starting transfers between devices  20.4 us (53%)
  waiting for transfers between devices  8.28 us (22%)
  Pallas kernels  7.84 us (21%)
  between operations  0.8 us (2%)
  other arithmetic  0.68 us (2%)
    ppermute x20, starting transfers between devices, swap(): return lax.ppermute(value, axis, [(i, i ^ dist) for i in range(size)])  20.4 us
    ppermute x20, waiting for transfers between devices, swap(): return lax.ppermute(value, axis, [(i, i ^ dist) for i in range(size)])  8.28 us
    pallas_call x1, Pallas kernels, shards(): pl.pallas_call(functools.partial(adjoint_kernel, dims, n_tile), out_shape...  3.64 us
    pallas_call x1, Pallas kernels, shards(): pl.pallas_call(functools.partial(forward_kernel, dims), out_shape=line_sh...  3.17 us
    pallas_call x1, Pallas kernels, shards(): pl.pallas_call(functools.partial(prior_kernel, dims, n_tile), out_shape=p...  1.03 us
  transfers between devices with their start and end apart: 20, of which 8 were waited for; matrix products, arithmetic and copies ran while one was open for 0% of the time, Pallas kernels for 11%

profile of v1, /device:TPU:0, one launch (start us, length us, event | category | flops | bytes accessed | tf_op | source)
XLA Modules:
  0.0 38.1 jit_solution(12537764436693168482)
XLA Ops:
  0.6 0.0 slice-start
  0.6 0.0 slice-start.1
  0.7 4.0 %collective-permute-start.5 = (f32[128,128]{1,0:T(8,128)}, f32[128,128]{1,0:T(8,128)S(1)}, u32[]{:S(2)}, u32[]{:S(2)}) collective-permute-start(f32[128,128]{1,0:T(8,128)} %bitcast.14), channel_id=1, source_target_pairs={{0,24},{4,28},{8,16},{12,20},{16,8},{20,12},{24,0},{28,4},{1,25},{... | collective-permute-start | bytes 196616 | tf_op jit(solution)/shard_map/ppermute | solution.py:200
  4.7 0.5 %collective-permute-start.3 = (f32[128,128]{1,0:T(8,128)}, f32[128,128]{1,0:T(8,128)S(1)}, u32[]{:S(2)}, u32[]{:S(2)}) collective-permute-start(f32[128,128]{1,0:T(8,128)} %bitcast.15), channel_id=1, source_target_pairs={{0,16},{4,20},{8,24},{12,28},{16,0},{20,4},{24,8},{28,12},{1,17},{... | collective-permute-start | bytes 196616 | tf_op jit(solution)/shard_map/ppermute | solution.py:200
  5.2 0.1 collective-permute-start.1
  5.3 0.0 collective-permute-start
  5.3 1.8 %collective-permute-done.5.refs_8_ = f32[128,128]{1,0:T(8,128)S(1)} collective-permute-done((f32[128,128]{1,0:T(8,128)}, f32[128,128]{1,0:T(8,128)S(1)}, u32[]{:S(2)}, u32[]{:S(2)}) %collective-permute-start.5) | collective-permute-done | bytes 65568 | tf_op jit(solution)/shard_map/ppermute | solution.py:200
  7.1 0.0 collective-permute-start.6
  7.1 4.1 %collective-permute-start.12 = (f32[128,128]{1,0:T(8,128)}, f32[128,128]{1,0:T(8,128)S(1)}, u32[]{:S(2)}, u32[]{:S(2)}) collective-permute-start(f32[128,128]{1,0:T(8,128)} %bitcast.18), channel_id=1, source_target_pairs={{0,3},{1,2},{2,1},{3,0},{4,7},{5,6},{6,5},{7,4},{8,11},{9,10},{10,... | collective-permute-start | bytes 196616 | tf_op jit(solution)/shard_map/ppermute | solution.py:200
  11.3 0.0 collective-permute-done.3.refs_6_
  11.3 0.5 %collective-permute-start.11 = (f32[128,128]{1,0:T(8,128)}, f32[128,128]{1,0:T(8,128)S(1)}, u32[]{:S(2)}, u32[]{:S(2)}) collective-permute-start(f32[128,128]{1,0:T(8,128)} %bitcast.19), channel_id=1, source_target_pairs={{0,2},{1,3},{2,0},{3,1},{4,6},{5,7},{6,4},{7,5},{8,10},{9,11},{10,... | collective-permute-start | bytes 196616 | tf_op jit(solution)/shard_map/ppermute | solution.py:200
  11.7 0.0 collective-permute-done.1.refs_4_
  11.7 1.6 %collective-permute-start.10 = (f32[128,128]{1,0:T(8,128)}, f32[128,128]{1,0:T(8,128)S(1)}, u32[]{:S(2)}, u32[]{:S(2)}) collective-permute-start(f32[128,128]{1,0:T(8,128)} %bitcast.20), channel_id=1, source_target_pairs={{0,1},{1,0},{2,3},{3,2},{4,5},{5,4},{6,7},{7,6},{8,9},{9,8},{10,11... | collective-permute-start | bytes 196616 | tf_op jit(solution)/shard_map/ppermute | solution.py:200
  13.3 0.0 collective-permute-done.refs_3_
  13.3 0.0 collective-permute-start.4
  13.3 0.0 collective-permute-done.6.refs_9_
  13.3 0.5 %collective-permute-start.2 = (f32[128,128]{1,0:T(8,128)S(1)}, f32[128,128]{1,0:T(8,128)S(1)}, u32[]{:S(2)}, u32[]{:S(2)}) collective-permute-start(f32[128,128]{1,0:T(8,128)S(1)} %collective-permute-done.1.refs_4_), channel_id=1, source_target_pairs={{0,4},{4,0},{8,12},{12,8},{16,20},{20,16},{24,28},{28,24},{1,5},{5... | collective-permute-start | bytes 196616 | tf_op jit(solution)/shard_map/ppermute | solution.py:200
  13.8 0.0 copy-start.6
  13.9 0.0 copy-start.7
  13.9 0.0 copy-start.8
  13.9 0.7 %collective-permute-done.4.refs_7_ = f32[128,128]{1,0:T(8,128)S(1)} collective-permute-done((f32[128,128]{1,0:T(8,128)S(1)}, f32[128,128]{1,0:T(8,128)S(1)}, u32[]{:S(2)}, u32[]{:S(2)}) %collective-permute-start.4) | collective-permute-done | bytes 65568 | tf_op jit(solution)/shard_map/ppermute | solution.py:200
  14.6 0.2 collective-permute-done.2.refs_5_
  14.8 3.2 %shard_map.114.refs_1_ = f32[1,256]{1,0:T(1,128)S(1)} custom-call(s32[2,256]{1,0:T(2,128)S(1)} %bitcast.23, s32[256]{0:T(256)S(1)} %copy-done.5, bf16[256,2,8,8,128]{4,3,2,1,0:T(8,128)(2,1)S(1)} %bitcast.12, f32[8,128]{1,0:T(8,128)S(1)} %shard_map.113.refs_1_, f32[128,128]{1,0:T(8,128)S(1)} %bitcast.21, f32[128,128]{1,0:T(8,128)S(1)} %collective-permute-done.refs_3_, ...), custom_call_target="tpu_custom_call" | custom-call | tf_op jit(solution)/shard_map/pallas_call | solution.py:222
  17.9 2.4 %collective-permute-start.9 = (f32[1,256]{1,0:T(1,128)S(1)}, f32[1,256]{1,0:T(1,128)S(1)}, u32[]{:S(2)}, u32[]{:S(2)}) collective-permute-start(f32[1,256]{1,0:T(1,128)S(1)} %shard_map.114.refs_1_), channel_id=1, source_target_pairs={{0,3},{1,2},{2,1},{3,0},{4,7},{5,6},{6,5},{7,4},{8,11},{9,10},{10,... | collective-permute-start | bytes 3080 | tf_op jit(solution)/shard_map/ppermute | solution.py:200
  20.3 0.0 collective-permute-start.8
  20.3 0.0 collective-permute-done.12.refs_3_
  20.3 2.0 %collective-permute-start.7 = (f32[1,256]{1,0:T(1,128)S(1)}, f32[1,256]{1,0:T(1,128)S(1)}, u32[]{:S(2)}, u32[]{:S(2)}) collective-permute-start(f32[1,256]{1,0:T(1,128)S(1)} %shard_map.114.refs_1_), channel_id=1, source_target_pairs={{0,1},{1,0},{2,3},{3,2},{4,5},{5,4},{6,7},{7,6},{8,9},{9,8},{10,11... | collective-permute-start | bytes 3080 | tf_op jit(solution)/shard_map/ppermute | solution.py:200
  22.4 0.0 collective-permute-done.11.refs_2_
  22.4 0.0 collective-permute-done.10.refs_1_
  22.4 1.0 %shard_map.115.refs_8_ = f32[1024,128]{1,0:T(8,128)S(1)} custom-call(f32[128,128]{1,0:T(8,128)S(1)} %bitcast.22, f32[128,128]{1,0:T(8,128)S(1)} %collective-permute-done.10.refs_1_, f32[128,128]{1,0:T(8,128)S(1)} %collective-permute-done.11.refs_2_, f32[128,128]{1,0:T(8,128)S(1)} %collective-permute-done.12.refs_3_, f32[128,512]{1,0:T(8,128)S(1)} %copy-done.1, ...), custom_call_target="tpu_custom_call" | custom-call | tf_op jit(solution)/shard_map/pallas_call | solution.py:231
  23.4 0.0 collective-permute-done.9.refs_4_
  23.4 1.3 %collective-permute-done.8.refs_3_ = f32[1,256]{1,0:T(1,128)S(1)} collective-permute-done((f32[1,256]{1,0:T(1,128)S(1)}, f32[1,256]{1,0:T(1,128)S(1)}, u32[]{:S(2)}, u32[]{:S(2)}) %collective-permute-start.8) | collective-permute-done | bytes 1056 | tf_op jit(solution)/shard_map/ppermute | solution.py:200
  24.8 0.0 collective-permute-done.7.refs_2_
  24.8 3.6 %shard_map.116 = (f32[128,128]{1,0:T(8,128)S(1)}, f32[128,128]{1,0:T(8,128)S(1)}, f32[128,128]{1,0:T(8,128)S(1)}, f32[128,128]{1,0:T(8,128)S(1)}, f32[128,128]{1...) custom-call(s32[2,256]{1,0:T(2,128)S(1)} %bitcast.24, ...), custom_call_target="tpu_custom_call" | custom-call | tf_op jit(solution)/shard_map/pallas_call | solution.py:239
  28.4 0.0 collective-permute-start.13
  28.5 0.5 %collective-permute-start.15 = (f32[128,128]{1,0:T(8,128)S(1)}, f32[128,128]{1,0:T(8,128)S(1)}, u32[]{:S(2)}, u32[]{:S(2)}) collective-permute-start(f32[128,128]{1,0:T(8,128)S(1)} %get-tuple-element.14), channel_id=1, source_target_pairs={{0,4},{4,0},{8,12},{12,8},{16,20},{20,16},{24,28},{28,24},{1,5},{5... | collective-permute-start | bytes 196616 | tf_op jit(solution)/shard_map/ppermute | solution.py:200
  29.0 0.0 collective-permute-start.17
  29.0 0.5 %collective-permute-start.19 = (f32[128,128]{1,0:T(8,128)S(1)}, f32[128,128]{1,0:T(8,128)S(1)}, u32[]{:S(2)}, u32[]{:S(2)}) collective-permute-start(f32[128,128]{1,0:T(8,128)S(1)} %get-tuple-element.18), channel_id=1, source_target_pairs={{0,4},{4,0},{8,12},{12,8},{16,20},{20,16},{24,28},{28,24},{1,5},{5... | collective-permute-start | bytes 196616 | tf_op jit(solution)/shard_map/ppermute | solution.py:200
  29.5 0.2 collective-permute-done.13
  29.7 2.7 %collective-permute-start.14 = (f32[128,128]{1,0:T(8,128)S(1)}, f32[128,128]{1,0:T(8,128)S(1)}, u32[]{:S(2)}, u32[]{:S(2)}) collective-permute-start(f32[128,128]{1,0:T(8,128)S(1)} %add.21), channel_id=1, source_target_pairs={{0,24},{4,28},{8,16},{12,20},{16,8},{20,12},{24,0},{28,4},{1,25},{... | collective-permute-start | bytes 196616 | tf_op jit(solution)/shard_map/ppermute | solution.py:200
  32.5 0.0 collective-permute-done.15
  32.5 0.6 %collective-permute-start.16 = (f32[128,128]{1,0:T(8,128)S(1)}, f32[128,128]{1,0:T(8,128)S(1)}, u32[]{:S(2)}, u32[]{:S(2)}) collective-permute-start(f32[128,128]{1,0:T(8,128)S(1)} %add.22), channel_id=1, source_target_pairs={{0,16},{4,20},{8,24},{12,28},{16,0},{20,4},{24,8},{28,12},{1,17},{... | collective-permute-start | bytes 196616 | tf_op jit(solution)/shard_map/ppermute | solution.py:200
  33.1 0.3 collective-permute-start.18
  33.4 0.0 collective-permute-done.19
  33.4 1.5 %collective-permute-done.14 = f32[128,128]{1,0:T(8,128)S(1)} collective-permute-done((f32[128,128]{1,0:T(8,128)S(1)}, f32[128,128]{1,0:T(8,128)S(1)}, u32[]{:S(2)}, u32[]{:S(2)}) %collective-permute-start.14) | collective-permute-done | bytes 65568 | tf_op jit(solution)/shard_map/ppermute | solution.py:200
  34.9 1.9 %collective-permute-done.16 = f32[128,128]{1,0:T(8,128)S(1)} collective-permute-done((f32[128,128]{1,0:T(8,128)S(1)}, f32[128,128]{1,0:T(8,128)S(1)}, u32[]{:S(2)}, u32[]{:S(2)}) %collective-permute-start.16) | collective-permute-done | bytes 65568 | tf_op jit(solution)/shard_map/ppermute | solution.py:200
  36.8 0.6 %collective-permute-done.18 = f32[128,128]{1,0:T(8,128)S(1)} collective-permute-done((f32[128,128]{1,0:T(8,128)S(1)}, f32[128,128]{1,0:T(8,128)S(1)}, u32[]{:S(2)}, u32[]{:S(2)}) %collective-permute-start.18) | collective-permute-done | bytes 65568 | tf_op jit(solution)/shard_map/ppermute | solution.py:200
  37.4 0.6 %add_add_fusion = f32[128,128]{1,0:T(8,128)} fusion(f32[128,128]{1,0:T(8,128)S(1)} %get-tuple-element.17, f32[128,128]{1,0:T(8,128)S(1)} %collective-permute-done.19, f32[128,128]{1,0:T(8,128)S(1)} %collective-permute-done.18, f32[128,128]{1,0:T(8,128)S(1)} %collective-permute-done.14, f32[128,128]{1,0:T(8,128)S(1)} %collective-permute-done.16), kind=kLoop, calls=%fused_computation | loop fusion | flops 65536 | bytes 393216 | tf_op jit(solution)/shard_map/add | solution.py:261
  (23 shorter events, 0.1 us)
Async XLA Ops:
  0.6 14.1 %slice-start = ((s8[8388608]{0:T(1024)(128)(4,1)}), s8[4194304]{0:T(1024)(128)(4,1)S(1)}, s32[]{:S(2)}) async-start(s8[8388608]{0:T(1024)(128)(4,1)} %bitcast.10), calls=%async_computation | async-start | bytes 8388608
  0.6 14.1 %slice-start.1 = ((s8[8388608]{0:T(1024)(128)(4,1)}), s8[4194304]{0:T(1024)(128)(4,1)S(1)}, s32[]{:S(2)}) async-start(s8[8388608]{0:T(1024)(128)(4,1)} %bitcast.10), calls=%async_computation.1 | async-start | bytes 8388608
  0.7 14.1 %copy-start = (f32[64,2,128]{2,1,0:T(2,128)S(1)}, f32[64,2,128]{2,1,0:T(2,128)}, u32[]{:S(2)}) copy-start(f32[64,2,128]{2,1,0:T(2,128)} %param.10) | copy-start | bytes 196612
  0.7 14.1 %copy-start.4 = (s32[256,1,2]{0,2,1:T(2,128)S(1)}, s32[256,1,2]{0,2,1:T(2,128)}, u32[]{:S(2)}) copy-start(s32[256,1,2]{0,2,1:T(2,128)} %param.12) | copy-start | bytes 6148
  0.7 14.1 %copy-start.5 = (s32[256]{0:T(256)S(1)}, s32[256]{0:T(256)}, u32[]{:S(2)}) copy-start(s32[256]{0:T(256)} %offset_ref.3) | copy-start | bytes 3076
  0.7 6.4 %collective-permute-start.5 = (f32[128,128]{1,0:T(8,128)}, f32[128,128]{1,0:T(8,128)S(1)}, u32[]{:S(2)}, u32[]{:S(2)}) collective-permute-start(f32[128,128]{1,0:T(8,128)} %bitcast.14), channel_id=1, source_target_pairs={{0,24},{4,28},{8,16},{12,20},{16,8},{20,12},{24,0},{28,4},{1,25},{... | collective-permute-start | bytes 196616 | tf_op jit(solution)/shard_map/ppermute | solution.py:200
  4.7 6.6 %collective-permute-start.3 = (f32[128,128]{1,0:T(8,128)}, f32[128,128]{1,0:T(8,128)S(1)}, u32[]{:S(2)}, u32[]{:S(2)}) collective-permute-start(f32[128,128]{1,0:T(8,128)} %bitcast.15), channel_id=1, source_target_pairs={{0,16},{4,20},{8,24},{12,28},{16,0},{20,4},{24,8},{28,12},{1,17},{... | collective-permute-start | bytes 196616 | tf_op jit(solution)/shard_map/ppermute | solution.py:200
  5.2 6.6 %collective-permute-start.1 = (f32[128,128]{1,0:T(8,128)}, f32[128,128]{1,0:T(8,128)S(1)}, u32[]{:S(2)}, u32[]{:S(2)}) collective-permute-start(f32[128,128]{1,0:T(8,128)} %bitcast.16), channel_id=1, source_target_pairs={{0,8},{4,12},{8,0},{12,4},{16,24},{20,28},{24,16},{28,20},{1,9},{5... | collective-permute-start | bytes 196616 | tf_op jit(solution)/shard_map/ppermute | solution.py:200
  5.3 8.0 %collective-permute-start = (f32[128,128]{1,0:T(8,128)}, f32[128,128]{1,0:T(8,128)S(1)}, u32[]{:S(2)}, u32[]{:S(2)}) collective-permute-start(f32[128,128]{1,0:T(8,128)} %bitcast.17), channel_id=1, source_target_pairs={{0,4},{4,0},{8,12},{12,8},{16,20},{20,16},{24,28},{28,24},{1,5},{5... | collective-permute-start | bytes 196616 | tf_op jit(solution)/shard_map/ppermute | solution.py:200
  7.1 6.2 %collective-permute-start.6 = (f32[128,128]{1,0:T(8,128)S(1)}, f32[128,128]{1,0:T(8,128)S(1)}, u32[]{:S(2)}, u32[]{:S(2)}) collective-permute-start(f32[128,128]{1,0:T(8,128)S(1)} %collective-permute-done.5.refs_8_), channel_id=1, source_target_pairs={{0,4},{4,0},{8,12},{12,8},{16,20},{20,16},{24,28},{28,24},{1,5},{5... | collective-permute-start | bytes 196616 | tf_op jit(solution)/shard_map/ppermute | solution.py:200
  7.1 13.2 %collective-permute-start.12 = (f32[128,128]{1,0:T(8,128)}, f32[128,128]{1,0:T(8,128)S(1)}, u32[]{:S(2)}, u32[]{:S(2)}) collective-permute-start(f32[128,128]{1,0:T(8,128)} %bitcast.18), channel_id=1, source_target_pairs={{0,3},{1,2},{2,1},{3,0},{4,7},{5,6},{6,5},{7,4},{8,11},{9,10},{10,... | collective-permute-start | bytes 196616 | tf_op jit(solution)/shard_map/ppermute | solution.py:200
  11.3 11.1 %collective-permute-start.11 = (f32[128,128]{1,0:T(8,128)}, f32[128,128]{1,0:T(8,128)S(1)}, u32[]{:S(2)}, u32[]{:S(2)}) collective-permute-start(f32[128,128]{1,0:T(8,128)} %bitcast.19), channel_id=1, source_target_pairs={{0,2},{1,3},{2,0},{3,1},{4,6},{5,7},{6,4},{7,5},{8,10},{9,11},{10,... | collective-permute-start | bytes 196616 | tf_op jit(solution)/shard_map/ppermute | solution.py:200
  11.7 10.6 %collective-permute-start.10 = (f32[128,128]{1,0:T(8,128)}, f32[128,128]{1,0:T(8,128)S(1)}, u32[]{:S(2)}, u32[]{:S(2)}) collective-permute-start(f32[128,128]{1,0:T(8,128)} %bitcast.20), channel_id=1, source_target_pairs={{0,1},{1,0},{2,3},{3,2},{4,5},{5,4},{6,7},{7,6},{8,9},{9,8},{10,11... | collective-permute-start | bytes 196616 | tf_op jit(solution)/shard_map/ppermute | solution.py:200
  13.3 1.3 %collective-permute-start.4 = (f32[128,128]{1,0:T(8,128)S(1)}, f32[128,128]{1,0:T(8,128)S(1)}, u32[]{:S(2)}, u32[]{:S(2)}) collective-permute-start(f32[128,128]{1,0:T(8,128)S(1)} %collective-permute-done.3.refs_6_), channel_id=1, source_target_pairs={{0,4},{4,0},{8,12},{12,8},{16,20},{20,16},{24,28},{28,24},{1,5},{5... | collective-permute-start | bytes 196616 | tf_op jit(solution)/shard_map/ppermute | solution.py:200
  13.3 1.4 %collective-permute-start.2 = (f32[128,128]{1,0:T(8,128)S(1)}, f32[128,128]{1,0:T(8,128)S(1)}, u32[]{:S(2)}, u32[]{:S(2)}) collective-permute-start(f32[128,128]{1,0:T(8,128)S(1)} %collective-permute-done.1.refs_4_), channel_id=1, source_target_pairs={{0,4},{4,0},{8,12},{12,8},{16,20},{20,16},{24,28},{28,24},{1,5},{5... | collective-permute-start | bytes 196616 | tf_op jit(solution)/shard_map/ppermute | solution.py:200
  13.8 8.5 %copy-start.1 = (f32[128,512]{1,0:T(8,128)S(1)}, f32[128,512]{1,0:T(8,128)}, u32[]{:S(2)}) copy-start(f32[128,512]{1,0:T(8,128)} %refs_4_.1) | copy-start | bytes 786436
  13.8 8.5 %copy-start.2 = (f32[64,64]{1,0:T(8,128)S(1)}, f32[64,64]{1,0:T(8,128)}, u32[]{:S(2)}) copy-start(f32[64,64]{1,0:T(8,128)} %refs_5_.1) | copy-start | bytes 49156
  13.8 8.5 %copy-start.3 = (f32[16,16]{1,0:T(8,128)S(1)}, f32[16,16]{1,0:T(8,128)}, u32[]{:S(2)}) copy-start(f32[16,16]{1,0:T(8,128)} %refs_6_.1) | copy-start | bytes 3076
  13.8 10.9 %copy-start.6 = (f32[256]{0:T(256)S(1)}, f32[256]{0:T(256)}, u32[]{:S(2)}) copy-start(f32[256]{0:T(256)} %param.14) | copy-start | bytes 3076
  13.9 10.9 %copy-start.7 = (s32[256]{0:T(256)S(1)}, s32[256]{0:T(256)}, u32[]{:S(2)}) copy-start(s32[256]{0:T(256)} %param.15) | copy-start | bytes 3076
  13.9 10.9 %copy-start.8 = (f32[4]{0:T(128)S(1)}, f32[4]{0:T(128)}, u32[]{:S(2)}) copy-start(f32[4]{0:T(128)} %param.16) | copy-start | bytes 52
  17.9 5.5 %collective-permute-start.9 = (f32[1,256]{1,0:T(1,128)S(1)}, f32[1,256]{1,0:T(1,128)S(1)}, u32[]{:S(2)}, u32[]{:S(2)}) collective-permute-start(f32[1,256]{1,0:T(1,128)S(1)} %shard_map.114.refs_1_), channel_id=1, source_target_pairs={{0,3},{1,2},{2,1},{3,0},{4,7},{5,6},{6,5},{7,4},{8,11},{9,10},{10,... | collective-permute-start | bytes 3080 | tf_op jit(solution)/shard_map/ppermute | solution.py:200
  20.3 4.5 %collective-permute-start.8 = (f32[1,256]{1,0:T(1,128)S(1)}, f32[1,256]{1,0:T(1,128)S(1)}, u32[]{:S(2)}, u32[]{:S(2)}) collective-permute-start(f32[1,256]{1,0:T(1,128)S(1)} %shard_map.114.refs_1_), channel_id=1, source_target_pairs={{0,2},{1,3},{2,0},{3,1},{4,6},{5,7},{6,4},{7,5},{8,10},{9,11},{10,... | collective-permute-start | bytes 3080 | tf_op jit(solution)/shard_map/ppermute | solution.py:200
  20.3 4.5 %collective-permute-start.7 = (f32[1,256]{1,0:T(1,128)S(1)}, f32[1,256]{1,0:T(1,128)S(1)}, u32[]{:S(2)}, u32[]{:S(2)}) collective-permute-start(f32[1,256]{1,0:T(1,128)S(1)} %shard_map.114.refs_1_), channel_id=1, source_target_pairs={{0,1},{1,0},{2,3},{3,2},{4,5},{5,4},{6,7},{7,6},{8,9},{9,8},{10,11... | collective-permute-start | bytes 3080 | tf_op jit(solution)/shard_map/ppermute | solution.py:200
  28.4 1.3 %collective-permute-start.13 = (f32[128,128]{1,0:T(8,128)S(1)}, f32[128,128]{1,0:T(8,128)S(1)}, u32[]{:S(2)}, u32[]{:S(2)}) collective-permute-start(f32[128,128]{1,0:T(8,128)S(1)} %get-tuple-element.12), channel_id=1, source_target_pairs={{0,4},{4,0},{8,12},{12,8},{16,20},{20,16},{24,28},{28,24},{1,5},{5... | collective-permute-start | bytes 196616 | tf_op jit(solution)/shard_map/ppermute | solution.py:200
  28.5 4.0 %collective-permute-start.15 = (f32[128,128]{1,0:T(8,128)S(1)}, f32[128,128]{1,0:T(8,128)S(1)}, u32[]{:S(2)}, u32[]{:S(2)}) collective-permute-start(f32[128,128]{1,0:T(8,128)S(1)} %get-tuple-element.14), channel_id=1, source_target_pairs={{0,4},{4,0},{8,12},{12,8},{16,20},{20,16},{24,28},{28,24},{1,5},{5... | collective-permute-start | bytes 196616 | tf_op jit(solution)/shard_map/ppermute | solution.py:200
  29.0 4.1 %collective-permute-start.17 = (f32[128,128]{1,0:T(8,128)S(1)}, f32[128,128]{1,0:T(8,128)S(1)}, u32[]{:S(2)}, u32[]{:S(2)}) collective-permute-start(f32[128,128]{1,0:T(8,128)S(1)} %get-tuple-element.16), channel_id=1, source_target_pairs={{0,4},{4,0},{8,12},{12,8},{16,20},{20,16},{24,28},{28,24},{1,5},{5... | collective-permute-start | bytes 196616 | tf_op jit(solution)/shard_map/ppermute | solution.py:200
  29.0 4.5 %collective-permute-start.19 = (f32[128,128]{1,0:T(8,128)S(1)}, f32[128,128]{1,0:T(8,128)S(1)}, u32[]{:S(2)}, u32[]{:S(2)}) collective-permute-start(f32[128,128]{1,0:T(8,128)S(1)} %get-tuple-element.18), channel_id=1, source_target_pairs={{0,4},{4,0},{8,12},{12,8},{16,20},{20,16},{24,28},{28,24},{1,5},{5... | collective-permute-start | bytes 196616 | tf_op jit(solution)/shard_map/ppermute | solution.py:200
  29.7 5.2 %collective-permute-start.14 = (f32[128,128]{1,0:T(8,128)S(1)}, f32[128,128]{1,0:T(8,128)S(1)}, u32[]{:S(2)}, u32[]{:S(2)}) collective-permute-start(f32[128,128]{1,0:T(8,128)S(1)} %add.21), channel_id=1, source_target_pairs={{0,24},{4,28},{8,16},{12,20},{16,8},{20,12},{24,0},{28,4},{1,25},{... | collective-permute-start | bytes 196616 | tf_op jit(solution)/shard_map/ppermute | solution.py:200
  32.5 4.3 %collective-permute-start.16 = (f32[128,128]{1,0:T(8,128)S(1)}, f32[128,128]{1,0:T(8,128)S(1)}, u32[]{:S(2)}, u32[]{:S(2)}) collective-permute-start(f32[128,128]{1,0:T(8,128)S(1)} %add.22), channel_id=1, source_target_pairs={{0,16},{4,20},{8,24},{12,28},{16,0},{20,4},{24,8},{28,12},{1,17},{... | collective-permute-start | bytes 196616 | tf_op jit(solution)/shard_map/ppermute | solution.py:200
  33.1 4.3 %collective-permute-start.18 = (f32[128,128]{1,0:T(8,128)S(1)}, f32[128,128]{1,0:T(8,128)S(1)}, u32[]{:S(2)}, u32[]{:S(2)}) collective-permute-start(f32[128,128]{1,0:T(8,128)S(1)} %add.24), channel_id=1, source_target_pairs={{0,8},{4,12},{8,0},{12,4},{16,24},{20,28},{24,16},{28,20},{1,9},{5... | collective-permute-start | bytes 196616 | tf_op jit(solution)/shard_map/ppermute | solution.py:200

commit v2 on v1

--- a/solution.py
+++ b/solution.py
@@ -9,7 +9,7 @@
 
 
 GROUP = 8
-N_ACC = 4
+N_ACC = 2
 HIGHEST = lax.Precision.HIGHEST
 
 
@@ -29,18 +29,16 @@
     ones_ref[...] = jnp.ones(ones_ref.shape, jnp.float32)
 
 
-def window_start(dims, tile_ref, offset_ref, slot, receptor):
-    periods, tiles_y, tile_rows = dims[:3]
-    tile = tile_ref[slot, receptor]
-    tile = jnp.where(tile < 0, tiles_y, tile)
-    return pl.multiple_of((tile * periods + offset_ref[receptor]) * tile_rows, tile_rows)
-
-
 def forward_kernel(dims, tile_ref, offset_ref, *refs):
     periods, tiles_y, tile_rows, lat_dev, receptors, slots, window = dims
-    foot_ref, ones_ref, blocks = refs[0], refs[1], refs[2:-3]
-    out_ref, table, sums = refs[-3:]
+    foot_ref, ones_ref, blocks = refs[0], refs[1], refs[2:-6]
+    out_ref, start_ref, table, sums, mixed, sem = refs[-6:]
     lanes = table.shape[-1]
+    tile = tile_ref[...]
+    tile = jnp.where(tile < 0, tiles_y, tile)
+    mixed[...] = (tile * periods + offset_ref[...]) * tile_rows
+    copy = pltpu.make_async_copy(mixed, start_ref, sem)
+    copy.start()
     own = lax.axis_index("rec")
     for dist, block in enumerate(blocks):
         start = place(own ^ dist, dims)
@@ -56,17 +54,20 @@
             receptor = group * GROUP + item
             total = None
             for slot in range(slots):
-                start = window_start(dims, tile_ref, offset_ref, slot, receptor)
+                start = pl.multiple_of(start_ref[slot, receptor], tile_rows)
                 field = table[pl.ds(start, window * tile_rows), :]
                 field = field.reshape(window, tile_rows, lanes)
                 block = foot_ref[receptor, slot].astype(jnp.float32)
                 part = jnp.sum(block * field, axis=0)
                 total = part if total is None else total + part
-            sums[receptor] = total
-        return carry
-
+            sums[pl.ds(pl.multiple_of(receptor * tile_rows, tile_rows), tile_rows), :] = total
+        return carry
+
+    copy.wait()
     lax.fori_loop(0, receptors // GROUP, step, 0)
-    rows = jnp.sum(sums[...], axis=1)
+    rows = sums[pl.ds(0, receptors, stride=tile_rows), :]
+    for row in range(1, tile_rows):
+        rows = rows + sums[pl.ds(row, receptors, stride=tile_rows), :]
     flat = dot(ones_ref[...], rows, ((1,), (1,)))
     out_ref[...] = flat[0:1, :]
 
@@ -110,7 +111,7 @@
     lax.fori_loop(0, periods, finish, 0, unroll=8)
 
 
-def adjoint_kernel(dims, n_tile, tile_ref, offset_ref, *refs):
+def adjoint_kernel(dims, n_tile, start_ref, *refs):
     periods, tiles_y, tile_rows, lat_dev, receptors, slots, window = dims
     foot_ref, refs = refs[0], refs[1:]
     preds = refs[:n_tile]
@@ -130,17 +131,18 @@
     for index in range(var_ref.shape[1]):
         variance = jnp.where(group == index, var_ref[:, index : index + 1], variance)
     misfit = (predicted - observed_ref[...]) / variance
-    misfit_ref[...] = misfit
+    misfit_ref[...] = jnp.broadcast_to(misfit, misfit_ref.shape)
     weight[...] = jnp.transpose(jnp.broadcast_to(misfit, (lanes, receptors)))
+    size = tiles_y * periods * tile_rows
     for acc in accs:
-        acc[...] = jnp.zeros(acc.shape, jnp.float32)
+        acc[pl.ds(0, size), :] = jnp.zeros((size, lanes), jnp.float32)
 
     def step(group, carry):
         for item in range(GROUP):
             receptor = group * GROUP + item
             scale = jnp.broadcast_to(weight[pl.ds(receptor, 1), :], (tile_rows, lanes))
             for slot in range(slots):
-                start = window_start(dims, tile_ref, offset_ref, slot, receptor)
+                start = pl.multiple_of(start_ref[slot, receptor], tile_rows)
                 acc = accs[(item * slots + slot) % len(accs)]
                 block = foot_ref[receptor, slot].astype(jnp.float32) * scale[None]
                 acc[pl.ds(start, window * tile_rows), :] += block.reshape(window * tile_rows, lanes)
@@ -148,7 +150,6 @@
 
     lax.fori_loop(0, receptors // GROUP, step, 0)
     total = accs[0]
-    size = tiles_y * periods * tile_rows
     chunk = 8 * tile_rows
 
     def finish(index, carry):
@@ -217,16 +218,20 @@
         compiler_params=pltpu.CompilerParams(vmem_limit_bytes=2**20),
         cost_estimate=pl.CostEstimate(flops=10**10, bytes_accessed=2 * 10**7, transcendentals=0),
     )()
-    tiles = tile_list[:, 0, :].T
     foot = footprint[:, 0]
-    partial_pred = pl.pallas_call(
+    partial_pred, starts = pl.pallas_call(
         functools.partial(forward_kernel, dims),
-        out_shape=line_shape,
-        in_specs=[smem] * 2 + [vmem] * (2 + n_rec),
-        out_specs=vmem,
-        scratch_shapes=[table_shape, pltpu.VMEM((receptors, tile_rows, lon_dev), jnp.float32)],
+        out_shape=[line_shape, pltpu.SMEM((slots, receptors), jnp.int32)],
+        in_specs=[vmem] * (4 + n_rec),
+        out_specs=[vmem, smem],
+        scratch_shapes=[
+            table_shape,
+            pltpu.VMEM((receptors * tile_rows, lon_dev), jnp.float32),
+            pltpu.VMEM((slots, receptors), jnp.int32),
+            pltpu.SemaphoreType.DMA,
+        ],
         compiler_params=params,
-    )(tiles, offset, foot, ones, *blocks)
+    )(tile_list[:, 0, :].T, offset.reshape(1, receptors), foot, ones, *blocks)
     preds = [partial_pred] + [swap(partial_pred, "tile", d) for d in range(1, n_tile)]
     prior = pl.pallas_call(
         functools.partial(prior_kernel, dims, n_tile),
@@ -238,14 +243,13 @@
     )(*strips, inv_lon, inv_time, inv_lat)
     results = pl.pallas_call(
         functools.partial(adjoint_kernel, dims, n_tile),
-        out_shape=[block_shape] * n_rec + [line_shape],
-        in_specs=[smem] * 2 + [vmem] * (n_tile + 5),
+        out_shape=[block_shape] * n_rec + [jax.ShapeDtypeStruct((8, receptors), jnp.float32)],
+        in_specs=[smem] + [vmem] * (n_tile + 5),
         out_specs=[vmem] * (n_rec + 1),
         scratch_shapes=[pltpu.VMEM((receptors, lon_dev), jnp.float32)] + [table_shape] * N_ACC,
         compiler_params=params,
     )(
-        tiles,
-        offset,
+        starts,
         foot,
         *preds,
         observed.reshape(1, receptors),
@@ -253,7 +257,7 @@
         group_var.reshape(1, -1),
         prior,
     )
-    misfit = results[n_rec].reshape(receptors)
+    misfit = results[n_rec][0]
     gradient = None
     for dist in list(reversed(range(2, n_rec, 2))) + [0]:
         value = results[dist] + swap(results[dist + 1], "rec", 1)

time: 38.2 us -> 37 us (0.969)
  Pallas kernels: 7.84 us -> 6.49 us
  local copies, waits for them, and re-layouts: 0.05 us -> 0.61 us
  waiting for transfers between devices: 8.28 us -> 7.74 us
    pallas_call x1, Pallas kernels: 3.64 us -> 2.49 us  [shards(): pl.pallas_call(functools.partial(adjoint_kernel, dims, n_tile), out_shape...]
    slice x0 -> x1, local copies, waits for them, and re-layouts: none -> 0.56 us  [shards(): misfit = results[n_rec][0]]
    ppermute x20, waiting for transfers between devices: 8.28 us -> 7.74 us  [swap(): return lax.ppermute(value, axis, [(i, i ^ dist) for i in range(size)])]
  transfers between devices with their start and end apart: 20 -> 20, of which waited for: 8 -> 8; matrix products, arithmetic and copies ran while one was open for 0% -> 2% of each run, Pallas kernels for 11% -> 11%
where the time goes in v2:
time: 37 us; the launch traced here: 36.9 us
  starting transfers between devices  20.5 us (55%)
  waiting for transfers between devices  7.74 us (21%)
  Pallas kernels  6.49 us (18%)
  between operations  0.82 us (2%)
  other arithmetic  0.68 us (2%)
  local copies, waits for them, and re-layouts  0.61 us (2%)
    ppermute x20, starting transfers between devices, swap(): return lax.ppermute(value, axis, [(i, i ^ dist) for i in range(size)])  20.5 us
    ppermute x20, waiting for transfers between devices, swap(): return lax.ppermute(value, axis, [(i, i ^ dist) for i in range(size)])  7.74 us
    pallas_call x1, Pallas kernels, shards(): pl.pallas_call(functools.partial(forward_kernel, dims), out_shape=[line_s...  2.97 us
    pallas_call x1, Pallas kernels, shards(): pl.pallas_call(functools.partial(adjoint_kernel, dims, n_tile), out_shape...  2.49 us
    pallas_call x1, Pallas kernels, shards(): pl.pallas_call(functools.partial(prior_kernel, dims, n_tile), out_shape=p...  1.03 us
  transfers between devices with their start and end apart: 20, of which 8 were waited for; matrix products, arithmetic and copies ran while one was open for 2% of the time, Pallas kernels for 11%

profile of v2, /device:TPU:0, one launch (start us, length us, event | category | flops | bytes accessed | tf_op | source)
XLA Modules:
  0.0 36.9 jit_solution(3805825198795386255)
XLA Ops:
  0.6 0.0 slice-start
  0.6 0.0 slice-start.1
  0.7 4.0 %collective-permute-start.5 = (f32[128,128]{1,0:T(8,128)}, f32[128,128]{1,0:T(8,128)S(1)}, u32[]{:S(2)}, u32[]{:S(2)}) collective-permute-start(f32[128,128]{1,0:T(8,128)} %bitcast.15), channel_id=1, source_target_pairs={{0,24},{4,28},{8,16},{12,20},{16,8},{20,12},{24,0},{28,4},{1,25},{... | collective-permute-start | bytes 196616 | tf_op jit(solution)/shard_map/ppermute | solution.py:201
  4.7 0.5 %collective-permute-start.3 = (f32[128,128]{1,0:T(8,128)}, f32[128,128]{1,0:T(8,128)S(1)}, u32[]{:S(2)}, u32[]{:S(2)}) collective-permute-start(f32[128,128]{1,0:T(8,128)} %bitcast.16), channel_id=1, source_target_pairs={{0,16},{4,20},{8,24},{12,28},{16,0},{20,4},{24,8},{28,12},{1,17},{... | collective-permute-start | bytes 196616 | tf_op jit(solution)/shard_map/ppermute | solution.py:201
  5.2 0.1 collective-permute-start.1
  5.3 0.0 collective-permute-start
  5.3 1.8 %collective-permute-done.5.refs_8_ = f32[128,128]{1,0:T(8,128)S(1)} collective-permute-done((f32[128,128]{1,0:T(8,128)}, f32[128,128]{1,0:T(8,128)S(1)}, u32[]{:S(2)}, u32[]{:S(2)}) %collective-permute-start.5) | collective-permute-done | bytes 65568 | tf_op jit(solution)/shard_map/ppermute | solution.py:201
  7.1 0.0 collective-permute-start.6
  7.1 4.1 %collective-permute-start.12 = (f32[128,128]{1,0:T(8,128)}, f32[128,128]{1,0:T(8,128)S(1)}, u32[]{:S(2)}, u32[]{:S(2)}) collective-permute-start(f32[128,128]{1,0:T(8,128)} %bitcast.19), channel_id=1, source_target_pairs={{0,3},{1,2},{2,1},{3,0},{4,7},{5,6},{6,5},{7,4},{8,11},{9,10},{10,... | collective-permute-start | bytes 196616 | tf_op jit(solution)/shard_map/ppermute | solution.py:201
  11.3 0.0 collective-permute-done.3.refs_6_
  11.3 0.5 %collective-permute-start.11 = (f32[128,128]{1,0:T(8,128)}, f32[128,128]{1,0:T(8,128)S(1)}, u32[]{:S(2)}, u32[]{:S(2)}) collective-permute-start(f32[128,128]{1,0:T(8,128)} %bitcast.20), channel_id=1, source_target_pairs={{0,2},{1,3},{2,0},{3,1},{4,6},{5,7},{6,4},{7,5},{8,10},{9,11},{10,... | collective-permute-start | bytes 196616 | tf_op jit(solution)/shard_map/ppermute | solution.py:201
  11.7 0.0 collective-permute-done.1.refs_4_
  11.7 1.6 %collective-permute-start.10 = (f32[128,128]{1,0:T(8,128)}, f32[128,128]{1,0:T(8,128)S(1)}, u32[]{:S(2)}, u32[]{:S(2)}) collective-permute-start(f32[128,128]{1,0:T(8,128)} %bitcast.21), channel_id=1, source_target_pairs={{0,1},{1,0},{2,3},{3,2},{4,5},{5,4},{6,7},{7,6},{8,9},{9,8},{10,11... | collective-permute-start | bytes 196616 | tf_op jit(solution)/shard_map/ppermute | solution.py:201
  13.3 0.0 collective-permute-done.refs_3_
  13.3 0.0 collective-permute-start.4
  13.3 0.0 collective-permute-done.6.refs_9_
  13.3 0.5 %collective-permute-start.2 = (f32[128,128]{1,0:T(8,128)S(1)}, f32[128,128]{1,0:T(8,128)S(1)}, u32[]{:S(2)}, u32[]{:S(2)}) collective-permute-start(f32[128,128]{1,0:T(8,128)S(1)} %collective-permute-done.1.refs_4_), channel_id=1, source_target_pairs={{0,4},{4,0},{8,12},{12,8},{16,20},{20,16},{24,28},{28,24},{1,5},{5... | collective-permute-start | bytes 196616 | tf_op jit(solution)/shard_map/ppermute | solution.py:201
  13.8 0.0 copy-start.6
  13.9 0.0 copy-start.7
  13.9 0.0 copy-start.8
  13.9 0.7 %collective-permute-done.4.refs_7_ = f32[128,128]{1,0:T(8,128)S(1)} collective-permute-done((f32[128,128]{1,0:T(8,128)S(1)}, f32[128,128]{1,0:T(8,128)S(1)}, u32[]{:S(2)}, u32[]{:S(2)}) %collective-permute-start.4) | collective-permute-done | bytes 65568 | tf_op jit(solution)/shard_map/ppermute | solution.py:201
  14.6 0.2 collective-permute-done.2.refs_5_
  14.8 3.0 %shard_map.114 = (f32[1,256]{1,0:T(1,128)S(1)}, s32[2,256]{1,0:T(2,128)S(4)}) custom-call(s32[2,256]{1,0:T(2,128)S(1)} %bitcast.24, s32[1,256]{1,0:T(1,128)S(1)} %bitcast.25, bf16[256,2,8,8,128]{4,3,2,1,0:T(8,128)(2,1)S(1)} %bitcast.13, f32[8,128]{1,0:T(8,128)S(1)} %shard_map.113.refs_1_, f32[128,128]{1,0:T(8,128)S(1)} %bitcast.22, ...), custom_call_target="tpu_custom_call" | custom-call | tf_op jit(solution)/shard_map/pallas_call | solution.py:222
  17.7 2.4 %collective-permute-start.9 = (f32[1,256]{1,0:T(1,128)S(1)}, f32[1,256]{1,0:T(1,128)S(1)}, u32[]{:S(2)}, u32[]{:S(2)}) collective-permute-start(f32[1,256]{1,0:T(1,128)S(1)} %get-tuple-element.14.refs_1_), channel_id=1, source_target_pairs={{0,3},{1,2},{2,1},{3,0},{4,7},{5,6},{6,5},{7,4},{8,11},{9,10},{10,... | collective-permute-start | bytes 3080 | tf_op jit(solution)/shard_map/ppermute | solution.py:201
  20.2 0.0 collective-permute-start.8
  20.2 0.0 collective-permute-done.12.refs_3_
  20.2 2.0 %collective-permute-start.7 = (f32[1,256]{1,0:T(1,128)S(1)}, f32[1,256]{1,0:T(1,128)S(1)}, u32[]{:S(2)}, u32[]{:S(2)}) collective-permute-start(f32[1,256]{1,0:T(1,128)S(1)} %get-tuple-element.14.refs_1_), channel_id=1, source_target_pairs={{0,1},{1,0},{2,3},{3,2},{4,5},{5,4},{6,7},{7,6},{8,9},{9,8},{10,11... | collective-permute-start | bytes 3080 | tf_op jit(solution)/shard_map/ppermute | solution.py:201
  22.2 0.0 collective-permute-done.11.refs_2_
  22.2 0.0 collective-permute-done.10.refs_1_
  22.2 1.0 %shard_map.115.refs_8_ = f32[1024,128]{1,0:T(8,128)S(1)} custom-call(f32[128,128]{1,0:T(8,128)S(1)} %bitcast.23, f32[128,128]{1,0:T(8,128)S(1)} %collective-permute-done.10.refs_1_, f32[128,128]{1,0:T(8,128)S(1)} %collective-permute-done.11.refs_2_, f32[128,128]{1,0:T(8,128)S(1)} %collective-permute-done.12.refs_3_, f32[128,512]{1,0:T(8,128)S(1)} %copy-done.1, ...), custom_call_target="tpu_custom_call" | custom-call | tf_op jit(solution)/shard_map/pallas_call | solution.py:236
  23.3 1.3 %collective-permute-done.8.refs_3_ = f32[1,256]{1,0:T(1,128)S(1)} collective-permute-done((f32[1,256]{1,0:T(1,128)S(1)}, f32[1,256]{1,0:T(1,128)S(1)}, u32[]{:S(2)}, u32[]{:S(2)}) %collective-permute-start.8) | collective-permute-done | bytes 1056 | tf_op jit(solution)/shard_map/ppermute | solution.py:201
  24.6 0.0 collective-permute-done.7.refs_2_
  24.7 2.5 %shard_map.116 = (f32[128,128]{1,0:T(8,128)S(1)}, f32[128,128]{1,0:T(8,128)S(1)}, f32[128,128]{1,0:T(8,128)S(1)}, f32[128,128]{1,0:T(8,128)S(1)}, f32[128,128]{1...) custom-call(s32[2,256]{1,0:T(2,128)S(4)} %get-tuple-element.13.start, ...), custom_call_target="tpu_custom_call" | custom-call | tf_op jit(solution)/shard_map/pallas_call | solution.py:244
  27.1 0.1 collective-permute-start.13
  27.2 0.5 %collective-permute-start.15 = (f32[128,128]{1,0:T(8,128)S(1)}, f32[128,128]{1,0:T(8,128)S(1)}, u32[]{:S(2)}, u32[]{:S(2)}) collective-permute-start(f32[128,128]{1,0:T(8,128)S(1)} %get-tuple-element.18), channel_id=1, source_target_pairs={{0,4},{4,0},{8,12},{12,8},{16,20},{20,16},{24,28},{28,24},{1,5},{5... | collective-permute-start | bytes 196616 | tf_op jit(solution)/shard_map/ppermute | solution.py:201
  27.7 0.1 collective-permute-start.17
  27.8 0.4 %collective-permute-start.19 = (f32[128,128]{1,0:T(8,128)S(1)}, f32[128,128]{1,0:T(8,128)S(1)}, u32[]{:S(2)}, u32[]{:S(2)}) collective-permute-start(f32[128,128]{1,0:T(8,128)S(1)} %get-tuple-element.22), channel_id=1, source_target_pairs={{0,4},{4,0},{8,12},{12,8},{16,20},{20,16},{24,28},{28,24},{1,5},{5... | collective-permute-start | bytes 196616 | tf_op jit(solution)/shard_map/ppermute | solution.py:201
  28.2 0.2 collective-permute-done.13
  28.5 2.7 %collective-permute-start.14 = (f32[128,128]{1,0:T(8,128)S(1)}, f32[128,128]{1,0:T(8,128)S(1)}, u32[]{:S(2)}, u32[]{:S(2)}) collective-permute-start(f32[128,128]{1,0:T(8,128)S(1)} %add.21), channel_id=1, source_target_pairs={{0,24},{4,28},{8,16},{12,20},{16,8},{20,12},{24,0},{28,4},{1,25},{... | collective-permute-start | bytes 196616 | tf_op jit(solution)/shard_map/ppermute | solution.py:201
  31.2 0.0 collective-permute-done.15
  31.2 0.7 %collective-permute-start.16 = (f32[128,128]{1,0:T(8,128)S(1)}, f32[128,128]{1,0:T(8,128)S(1)}, u32[]{:S(2)}, u32[]{:S(2)}) collective-permute-start(f32[128,128]{1,0:T(8,128)S(1)} %add.22), channel_id=1, source_target_pairs={{0,16},{4,20},{8,24},{12,28},{16,0},{20,4},{24,8},{28,12},{1,17},{... | collective-permute-start | bytes 196616 | tf_op jit(solution)/shard_map/ppermute | solution.py:201
  31.9 0.3 collective-permute-start.18
  32.2 0.6 %slice.3 = f32[1,256]{1,0:T(1,128)} slice(f32[8,256]{1,0:T(8,128)S(1)} %get-tuple-element.23), slice={[0:1], [0:256]} | slice | bytes 2048 | tf_op jit(solution)/shard_map/slice | solution.py:260
  32.8 0.0 collective-permute-done.19
  32.8 0.9 %collective-permute-done.14 = f32[128,128]{1,0:T(8,128)S(1)} collective-permute-done((f32[128,128]{1,0:T(8,128)S(1)}, f32[128,128]{1,0:T(8,128)S(1)}, u32[]{:S(2)}, u32[]{:S(2)}) %collective-permute-start.14) | collective-permute-done | bytes 65568 | tf_op jit(solution)/shard_map/ppermute | solution.py:201
  33.7 1.9 %collective-permute-done.16 = f32[128,128]{1,0:T(8,128)S(1)} collective-permute-done((f32[128,128]{1,0:T(8,128)S(1)}, f32[128,128]{1,0:T(8,128)S(1)}, u32[]{:S(2)}, u32[]{:S(2)}) %collective-permute-start.16) | collective-permute-done | bytes 65568 | tf_op jit(solution)/shard_map/ppermute | solution.py:201
  35.6 0.7 %collective-permute-done.18 = f32[128,128]{1,0:T(8,128)S(1)} collective-permute-done((f32[128,128]{1,0:T(8,128)S(1)}, f32[128,128]{1,0:T(8,128)S(1)}, u32[]{:S(2)}, u32[]{:S(2)}) %collective-permute-start.18) | collective-permute-done | bytes 65568 | tf_op jit(solution)/shard_map/ppermute | solution.py:201
  36.2 0.7 %add_add_fusion = f32[128,128]{1,0:T(8,128)} fusion(f32[128,128]{1,0:T(8,128)S(1)} %get-tuple-element.21, f32[128,128]{1,0:T(8,128)S(1)} %collective-permute-done.19, f32[128,128]{1,0:T(8,128)S(1)} %collective-permute-done.18, f32[128,128]{1,0:T(8,128)S(1)} %collective-permute-done.14, f32[128,128]{1,0:T(8,128)S(1)} %collective-permute-done.16), kind=kLoop, calls=%fused_computation | loop fusion | flops 65536 | bytes 393216 | tf_op jit(solution)/shard_map/add | solution.py:265
  (24 shorter events, 0.1 us)
Async XLA Ops:
  0.6 14.1 %slice-start = ((s8[8388608]{0:T(1024)(128)(4,1)}), s8[4194304]{0:T(1024)(128)(4,1)S(1)}, s32[]{:S(2)}) async-start(s8[8388608]{0:T(1024)(128)(4,1)} %bitcast.11), calls=%async_computation | async-start | bytes 8388608
  0.6 14.1 %slice-start.1 = ((s8[8388608]{0:T(1024)(128)(4,1)}), s8[4194304]{0:T(1024)(128)(4,1)S(1)}, s32[]{:S(2)}) async-start(s8[8388608]{0:T(1024)(128)(4,1)} %bitcast.11), calls=%async_computation.1 | async-start | bytes 8388608
  0.7 14.1 %copy-start = (f32[64,2,128]{2,1,0:T(2,128)S(1)}, f32[64,2,128]{2,1,0:T(2,128)}, u32[]{:S(2)}) copy-start(f32[64,2,128]{2,1,0:T(2,128)} %param.10) | copy-start | bytes 196612
  0.7 14.1 %copy-start.4 = (s32[256,1,2]{0,2,1:T(2,128)S(1)}, s32[256,1,2]{0,2,1:T(2,128)}, u32[]{:S(2)}) copy-start(s32[256,1,2]{0,2,1:T(2,128)} %param.12) | copy-start | bytes 6148
  0.7 14.1 %copy-start.5 = (s32[256]{0:T(256)S(1)}, s32[256]{0:T(256)}, u32[]{:S(2)}) copy-start(s32[256]{0:T(256)} %param.13) | copy-start | bytes 3076
  0.7 6.4 %collective-permute-start.5 = (f32[128,128]{1,0:T(8,128)}, f32[128,128]{1,0:T(8,128)S(1)}, u32[]{:S(2)}, u32[]{:S(2)}) collective-permute-start(f32[128,128]{1,0:T(8,128)} %bitcast.15), channel_id=1, source_target_pairs={{0,24},{4,28},{8,16},{12,20},{16,8},{20,12},{24,0},{28,4},{1,25},{... | collective-permute-start | bytes 196616 | tf_op jit(solution)/shard_map/ppermute | solution.py:201
  4.7 6.6 %collective-permute-start.3 = (f32[128,128]{1,0:T(8,128)}, f32[128,128]{1,0:T(8,128)S(1)}, u32[]{:S(2)}, u32[]{:S(2)}) collective-permute-start(f32[128,128]{1,0:T(8,128)} %bitcast.16), channel_id=1, source_target_pairs={{0,16},{4,20},{8,24},{12,28},{16,0},{20,4},{24,8},{28,12},{1,17},{... | collective-permute-start | bytes 196616 | tf_op jit(solution)/shard_map/ppermute | solution.py:201
  5.2 6.6 %collective-permute-start.1 = (f32[128,128]{1,0:T(8,128)}, f32[128,128]{1,0:T(8,128)S(1)}, u32[]{:S(2)}, u32[]{:S(2)}) collective-permute-start(f32[128,128]{1,0:T(8,128)} %bitcast.17), channel_id=1, source_target_pairs={{0,8},{4,12},{8,0},{12,4},{16,24},{20,28},{24,16},{28,20},{1,9},{5... | collective-permute-start | bytes 196616 | tf_op jit(solution)/shard_map/ppermute | solution.py:201
  5.3 8.0 %collective-permute-start = (f32[128,128]{1,0:T(8,128)}, f32[128,128]{1,0:T(8,128)S(1)}, u32[]{:S(2)}, u32[]{:S(2)}) collective-permute-start(f32[128,128]{1,0:T(8,128)} %bitcast.18), channel_id=1, source_target_pairs={{0,4},{4,0},{8,12},{12,8},{16,20},{20,16},{24,28},{28,24},{1,5},{5... | collective-permute-start | bytes 196616 | tf_op jit(solution)/shard_map/ppermute | solution.py:201
  7.1 6.2 %collective-permute-start.6 = (f32[128,128]{1,0:T(8,128)S(1)}, f32[128,128]{1,0:T(8,128)S(1)}, u32[]{:S(2)}, u32[]{:S(2)}) collective-permute-start(f32[128,128]{1,0:T(8,128)S(1)} %collective-permute-done.5.refs_8_), channel_id=1, source_target_pairs={{0,4},{4,0},{8,12},{12,8},{16,20},{20,16},{24,28},{28,24},{1,5},{5... | collective-permute-start | bytes 196616 | tf_op jit(solution)/shard_map/ppermute | solution.py:201
  7.1 13.0 %collective-permute-start.12 = (f32[128,128]{1,0:T(8,128)}, f32[128,128]{1,0:T(8,128)S(1)}, u32[]{:S(2)}, u32[]{:S(2)}) collective-permute-start(f32[128,128]{1,0:T(8,128)} %bitcast.19), channel_id=1, source_target_pairs={{0,3},{1,2},{2,1},{3,0},{4,7},{5,6},{6,5},{7,4},{8,11},{9,10},{10,... | collective-permute-start | bytes 196616 | tf_op jit(solution)/shard_map/ppermute | solution.py:201
  11.3 10.9 %collective-permute-start.11 = (f32[128,128]{1,0:T(8,128)}, f32[128,128]{1,0:T(8,128)S(1)}, u32[]{:S(2)}, u32[]{:S(2)}) collective-permute-start(f32[128,128]{1,0:T(8,128)} %bitcast.20), channel_id=1, source_target_pairs={{0,2},{1,3},{2,0},{3,1},{4,6},{5,7},{6,4},{7,5},{8,10},{9,11},{10,... | collective-permute-start | bytes 196616 | tf_op jit(solution)/shard_map/ppermute | solution.py:201
  11.7 10.5 %collective-permute-start.10 = (f32[128,128]{1,0:T(8,128)}, f32[128,128]{1,0:T(8,128)S(1)}, u32[]{:S(2)}, u32[]{:S(2)}) collective-permute-start(f32[128,128]{1,0:T(8,128)} %bitcast.21), channel_id=1, source_target_pairs={{0,1},{1,0},{2,3},{3,2},{4,5},{5,4},{6,7},{7,6},{8,9},{9,8},{10,11... | collective-permute-start | bytes 196616 | tf_op jit(solution)/shard_map/ppermute | solution.py:201
  13.3 1.3 %collective-permute-start.4 = (f32[128,128]{1,0:T(8,128)S(1)}, f32[128,128]{1,0:T(8,128)S(1)}, u32[]{:S(2)}, u32[]{:S(2)}) collective-permute-start(f32[128,128]{1,0:T(8,128)S(1)} %collective-permute-done.3.refs_6_), channel_id=1, source_target_pairs={{0,4},{4,0},{8,12},{12,8},{16,20},{20,16},{24,28},{28,24},{1,5},{5... | collective-permute-start | bytes 196616 | tf_op jit(solution)/shard_map/ppermute | solution.py:201
  13.3 1.4 %collective-permute-start.2 = (f32[128,128]{1,0:T(8,128)S(1)}, f32[128,128]{1,0:T(8,128)S(1)}, u32[]{:S(2)}, u32[]{:S(2)}) collective-permute-start(f32[128,128]{1,0:T(8,128)S(1)} %collective-permute-done.1.refs_4_), channel_id=1, source_target_pairs={{0,4},{4,0},{8,12},{12,8},{16,20},{20,16},{24,28},{28,24},{1,5},{5... | collective-permute-start | bytes 196616 | tf_op jit(solution)/shard_map/ppermute | solution.py:201
  13.8 8.4 %copy-start.1 = (f32[128,512]{1,0:T(8,128)S(1)}, f32[128,512]{1,0:T(8,128)}, u32[]{:S(2)}) copy-start(f32[128,512]{1,0:T(8,128)} %refs_4_.1) | copy-start | bytes 786436
  13.8 8.4 %copy-start.2 = (f32[64,64]{1,0:T(8,128)S(1)}, f32[64,64]{1,0:T(8,128)}, u32[]{:S(2)}) copy-start(f32[64,64]{1,0:T(8,128)} %refs_5_.1) | copy-start | bytes 49156
  13.8 8.4 %copy-start.3 = (f32[16,16]{1,0:T(8,128)S(1)}, f32[16,16]{1,0:T(8,128)}, u32[]{:S(2)}) copy-start(f32[16,16]{1,0:T(8,128)} %refs_6_.1) | copy-start | bytes 3076
  13.8 10.8 %copy-start.6 = (f32[256]{0:T(256)S(1)}, f32[256]{0:T(256)}, u32[]{:S(2)}) copy-start(f32[256]{0:T(256)} %param.14) | copy-start | bytes 3076
  13.9 10.8 %copy-start.7 = (s32[256]{0:T(256)S(1)}, s32[256]{0:T(256)}, u32[]{:S(2)}) copy-start(s32[256]{0:T(256)} %param.15) | copy-start | bytes 3076
  13.9 10.8 %copy-start.8 = (f32[4]{0:T(128)S(1)}, f32[4]{0:T(128)}, u32[]{:S(2)}) copy-start(f32[4]{0:T(128)} %param.16) | copy-start | bytes 52
  17.7 5.5 %collective-permute-start.9 = (f32[1,256]{1,0:T(1,128)S(1)}, f32[1,256]{1,0:T(1,128)S(1)}, u32[]{:S(2)}, u32[]{:S(2)}) collective-permute-start(f32[1,256]{1,0:T(1,128)S(1)} %get-tuple-element.14.refs_1_), channel_id=1, source_target_pairs={{0,3},{1,2},{2,1},{3,0},{4,7},{5,6},{6,5},{7,4},{8,11},{9,10},{10,... | collective-permute-start | bytes 3080 | tf_op jit(solution)/shard_map/ppermute | solution.py:201
  20.2 4.5 %collective-permute-start.8 = (f32[1,256]{1,0:T(1,128)S(1)}, f32[1,256]{1,0:T(1,128)S(1)}, u32[]{:S(2)}, u32[]{:S(2)}) collective-permute-start(f32[1,256]{1,0:T(1,128)S(1)} %get-tuple-element.14.refs_1_), channel_id=1, source_target_pairs={{0,2},{1,3},{2,0},{3,1},{4,6},{5,7},{6,4},{7,5},{8,10},{9,11},{10,... | collective-permute-start | bytes 3080 | tf_op jit(solution)/shard_map/ppermute | solution.py:201
  20.2 4.5 %collective-permute-start.7 = (f32[1,256]{1,0:T(1,128)S(1)}, f32[1,256]{1,0:T(1,128)S(1)}, u32[]{:S(2)}, u32[]{:S(2)}) collective-permute-start(f32[1,256]{1,0:T(1,128)S(1)} %get-tuple-element.14.refs_1_), channel_id=1, source_target_pairs={{0,1},{1,0},{2,3},{3,2},{4,5},{5,4},{6,7},{7,6},{8,9},{9,8},{10,11... | collective-permute-start | bytes 3080 | tf_op jit(solution)/shard_map/ppermute | solution.py:201
  27.1 1.3 %collective-permute-start.13 = (f32[128,128]{1,0:T(8,128)S(1)}, f32[128,128]{1,0:T(8,128)S(1)}, u32[]{:S(2)}, u32[]{:S(2)}) collective-permute-start(f32[128,128]{1,0:T(8,128)S(1)} %get-tuple-element.16), channel_id=1, source_target_pairs={{0,4},{4,0},{8,12},{12,8},{16,20},{20,16},{24,28},{28,24},{1,5},{5... | collective-permute-start | bytes 196616 | tf_op jit(solution)/shard_map/ppermute | solution.py:201
  27.2 4.0 %collective-permute-start.15 = (f32[128,128]{1,0:T(8,128)S(1)}, f32[128,128]{1,0:T(8,128)S(1)}, u32[]{:S(2)}, u32[]{:S(2)}) collective-permute-start(f32[128,128]{1,0:T(8,128)S(1)} %get-tuple-element.18), channel_id=1, source_target_pairs={{0,4},{4,0},{8,12},{12,8},{16,20},{20,16},{24,28},{28,24},{1,5},{5... | collective-permute-start | bytes 196616 | tf_op jit(solution)/shard_map/ppermute | solution.py:201
  27.7 4.2 %collective-permute-start.17 = (f32[128,128]{1,0:T(8,128)S(1)}, f32[128,128]{1,0:T(8,128)S(1)}, u32[]{:S(2)}, u32[]{:S(2)}) collective-permute-start(f32[128,128]{1,0:T(8,128)S(1)} %get-tuple-element.20), channel_id=1, source_target_pairs={{0,4},{4,0},{8,12},{12,8},{16,20},{20,16},{24,28},{28,24},{1,5},{5... | collective-permute-start | bytes 196616 | tf_op jit(solution)/shard_map/ppermute | solution.py:201
  27.8 5.0 %collective-permute-start.19 = (f32[128,128]{1,0:T(8,128)S(1)}, f32[128,128]{1,0:T(8,128)S(1)}, u32[]{:S(2)}, u32[]{:S(2)}) collective-permute-start(f32[128,128]{1,0:T(8,128)S(1)} %get-tuple-element.22), channel_id=1, source_target_pairs={{0,4},{4,0},{8,12},{12,8},{16,20},{20,16},{24,28},{28,24},{1,5},{5... | collective-permute-start | bytes 196616 | tf_op jit(solution)/shard_map/ppermute | solution.py:201
  28.5 5.2 %collective-permute-start.14 = (f32[128,128]{1,0:T(8,128)S(1)}, f32[128,128]{1,0:T(8,128)S(1)}, u32[]{:S(2)}, u32[]{:S(2)}) collective-permute-start(f32[128,128]{1,0:T(8,128)S(1)} %add.21), channel_id=1, source_target_pairs={{0,24},{4,28},{8,16},{12,20},{16,8},{20,12},{24,0},{28,4},{1,25},{... | collective-permute-start | bytes 196616 | tf_op jit(solution)/shard_map/ppermute | solution.py:201
  31.2 4.3 %collective-permute-start.16 = (f32[128,128]{1,0:T(8,128)S(1)}, f32[128,128]{1,0:T(8,128)S(1)}, u32[]{:S(2)}, u32[]{:S(2)}) collective-permute-start(f32[128,128]{1,0:T(8,128)S(1)} %add.22), channel_id=1, source_target_pairs={{0,16},{4,20},{8,24},{12,28},{16,0},{20,4},{24,8},{28,12},{1,17},{... | collective-permute-start | bytes 196616 | tf_op jit(solution)/shard_map/ppermute | solution.py:201
  31.9 4.3 %collective-permute-start.18 = (f32[128,128]{1,0:T(8,128)S(1)}, f32[128,128]{1,0:T(8,128)S(1)}, u32[]{:S(2)}, u32[]{:S(2)}) collective-permute-start(f32[128,128]{1,0:T(8,128)S(1)} %add.24), channel_id=1, source_target_pairs={{0,8},{4,12},{8,0},{12,4},{16,24},{20,28},{24,16},{28,20},{1,9},{5... | collective-permute-start | bytes 196616 | tf_op jit(solution)/shard_map/ppermute | solution.py:201

commit v3 on v2

--- a/solution.py
+++ b/solution.py
@@ -29,18 +29,28 @@
     ones_ref[...] = jnp.ones(ones_ref.shape, jnp.float32)
 
 
-def forward_kernel(dims, tile_ref, offset_ref, *refs):
-    periods, tiles_y, tile_rows, lat_dev, receptors, slots, window = dims
-    foot_ref, ones_ref, blocks = refs[0], refs[1], refs[2:-6]
-    out_ref, start_ref, table, sums, mixed, sem = refs[-6:]
-    lanes = table.shape[-1]
+def index_kernel(dims, tile_ref, offset_ref, start_ref, mixed, sem):
+    periods, tiles_y, tile_rows = dims[:3]
     tile = tile_ref[...]
     tile = jnp.where(tile < 0, tiles_y, tile)
     mixed[...] = (tile * periods + offset_ref[...]) * tile_rows
     copy = pltpu.make_async_copy(mixed, start_ref, sem)
     copy.start()
+    copy.wait()
+
+
+def stack_kernel(ones_ref, *refs):
+    for index, block in enumerate(refs[:-1]):
+        refs[-1][index] = block[...]
+
+
+def forward_kernel(dims, start_ref, foot_ref, ones_ref, even_ref, odd_ref, *refs):
+    periods, tiles_y, tile_rows, lat_dev, receptors, slots, window = dims
+    out_ref, table, sums = refs
+    lanes = table.shape[-1]
     own = lax.axis_index("rec")
-    for dist, block in enumerate(blocks):
+    for dist in range(2 * even_ref.shape[0]):
+        block = (odd_ref if dist % 2 else even_ref).at[dist // 2]
         start = place(own ^ dist, dims)
         for row in range(lat_dev):
             table[pl.ds(start + row, periods, stride=tile_rows), :] = block[
@@ -63,7 +73,6 @@
             sums[pl.ds(pl.multiple_of(receptor * tile_rows, tile_rows), tile_rows), :] = total
         return carry
 
-    copy.wait()
     lax.fori_loop(0, receptors // GROUP, step, 0)
     rows = sums[pl.ds(0, receptors, stride=tile_rows), :]
     for row in range(1, tile_rows):
@@ -149,24 +158,14 @@
         return carry
 
     lax.fori_loop(0, receptors // GROUP, step, 0)
-    total = accs[0]
-    chunk = 8 * tile_rows
-
-    def finish(index, carry):
-        rows = pl.ds(pl.multiple_of(index * chunk, chunk), chunk)
-        value = prior_ref[rows, :]
-        for acc in accs:
-            value = value + acc[rows, :]
-        total[rows, :] = value
-        return carry
-
-    lax.fori_loop(0, size // chunk, finish, 0)
     for dist, out in enumerate(outs):
         start = place(own ^ dist, dims)
         for row in range(lat_dev):
-            out[pl.ds(row, periods, stride=lat_dev), :] = total[
-                pl.ds(start + row, periods, stride=tile_rows), :
-            ]
+            rows = pl.ds(start + row, periods, stride=tile_rows)
+            value = prior_ref[rows, :]
+            for acc in accs:
+                value = value + acc[rows, :]
+            out[pl.ds(row, periods, stride=lat_dev), :] = value
 
 
 def shards(
@@ -201,15 +200,7 @@
         return lax.ppermute(value, axis, [(i, i ^ dist) for i in range(size)])
 
     local = deviation.reshape(field_rows, lon_dev)
-    far = range(2, n_rec, 2)
-    even = {0: local}
-    for dist in far:
-        even[dist] = swap(local, "rec", dist)
-    blocks = []
-    for dist in range(0, n_rec, 2):
-        blocks += [even[dist], swap(even[dist], "rec", 1)]
-    strips = [local] + [swap(local, "tile", d) for d in range(1, n_tile)]
-
+    even = [local] + [swap(local, "rec", dist) for dist in range(2, n_rec, 2)]
     ones = pl.pallas_call(
         ones_kernel,
         out_shape=jax.ShapeDtypeStruct((8, lon_dev), jnp.float32),
@@ -218,20 +209,36 @@
         compiler_params=pltpu.CompilerParams(vmem_limit_bytes=2**20),
         cost_estimate=pl.CostEstimate(flops=10**10, bytes_accessed=2 * 10**7, transcendentals=0),
     )()
+    even = pl.pallas_call(
+        stack_kernel,
+        out_shape=jax.ShapeDtypeStruct((n_rec // 2, field_rows, lon_dev), jnp.float32),
+        in_specs=[vmem] * (n_rec // 2 + 1),
+        out_specs=vmem,
+        compiler_params=pltpu.CompilerParams(vmem_limit_bytes=8 * 2**20),
+    )(ones, *even)
+    odd = swap(even, "rec", 1)
+    strips = [local] + [swap(local, "tile", d) for d in range(1, n_tile)]
+
     foot = footprint[:, 0]
-    partial_pred, starts = pl.pallas_call(
+    starts = pl.pallas_call(
+        functools.partial(index_kernel, dims),
+        out_shape=pltpu.SMEM((slots, receptors), jnp.int32),
+        in_specs=[vmem] * 2,
+        out_specs=smem,
+        scratch_shapes=[pltpu.VMEM((slots, receptors), jnp.int32), pltpu.SemaphoreType.DMA],
+        compiler_params=pltpu.CompilerParams(vmem_limit_bytes=2**20),
+    )(tile_list[:, 0, :].T, offset.reshape(1, receptors))
+    partial_pred = pl.pallas_call(
         functools.partial(forward_kernel, dims),
-        out_shape=[line_shape, pltpu.SMEM((slots, receptors), jnp.int32)],
-        in_specs=[vmem] * (4 + n_rec),
-        out_specs=[vmem, smem],
+        out_shape=line_shape,
+        in_specs=[smem] + [vmem] * 4,
+        out_specs=vmem,
         scratch_shapes=[
             table_shape,
             pltpu.VMEM((receptors * tile_rows, lon_dev), jnp.float32),
-            pltpu.VMEM((slots, receptors), jnp.int32),
-            pltpu.SemaphoreType.DMA,
         ],
         compiler_params=params,
-    )(tile_list[:, 0, :].T, offset.reshape(1, receptors), foot, ones, *blocks)
+    )(starts, foot, ones, even, odd)
     preds = [partial_pred] + [swap(partial_pred, "tile", d) for d in range(1, n_tile)]
     prior = pl.pallas_call(
         functools.partial(prior_kernel, dims, n_tile),

time: 37 us -> 36.7 us (level)
  starting transfers between devices: 20.5 us -> 18.3 us
  waiting for transfers between devices: 7.74 us -> 9.45 us
    ppermute x20 -> x17, starting transfers between devices: 20.5 us -> 18.3 us  [swap(): return lax.ppermute(value, axis, [(i, i ^ dist) for i in range(size)])]
    ppermute x20 -> x17, waiting for transfers between devices: 7.74 us -> 9.45 us  [swap(): return lax.ppermute(value, axis, [(i, i ^ dist) for i in range(size)])]
    pallas_call x1 -> x3, Pallas kernels: 2.97 us -> 3.06 us  [the longest x1 2.46 us: shards(): pl.pallas_call(functools.partial(forward_kernel, dims), out_shape=line_sh...]
  transfers between devices with their start and end apart: 20 -> 17, of which waited for: 8 -> 8; matrix products, arithmetic and copies ran while one was open for 2% -> 2% of each run, Pallas kernels for 11% -> 11%
where the time goes in v3:
time: 36.7 us; the launch traced here: 36.5 us
  starting transfers between devices  18.3 us (50%)
  waiting for transfers between devices  9.45 us (26%)
  Pallas kernels  6.62 us (18%)
  between operations  0.84 us (2%)
  other arithmetic  0.68 us (2%)
  local copies, waits for them, and re-layouts  0.61 us (2%)
    ppermute x17, starting transfers between devices, swap(): return lax.ppermute(value, axis, [(i, i ^ dist) for i in range(size)])  18.3 us
    ppermute x17, waiting for transfers between devices, swap(): return lax.ppermute(value, axis, [(i, i ^ dist) for i in range(size)])  9.45 us
    pallas_call x1, Pallas kernels, shards(): pl.pallas_call(functools.partial(adjoint_kernel, dims, n_tile), out_shape...  2.53 us
    pallas_call x1, Pallas kernels, shards(): pl.pallas_call(functools.partial(forward_kernel, dims), out_shape=line_sh...  2.46 us
    pallas_call x1, Pallas kernels, shards(): pl.pallas_call(functools.partial(prior_kernel, dims, n_tile), out_shape=p...  1.03 us
  transfers between devices with their start and end apart: 17, of which 8 were waited for; matrix products, arithmetic and copies ran while one was open for 2% of the time, Pallas kernels for 11%

profile of v3, /device:TPU:0, one launch (start us, length us, event | category | flops | bytes accessed | tf_op | source)
XLA Modules:
  0.0 36.5 jit_solution(14278028688142749864)
XLA Ops:
  0.6 0.0 slice-start
  0.6 0.0 copy-start.1
  0.7 0.0 copy-start.4
  0.7 0.0 copy-start.5
  0.7 0.0 slice-start.1
  0.7 4.0 %collective-permute-start.2 = (f32[128,128]{1,0:T(8,128)}, f32[128,128]{1,0:T(8,128)S(1)}, u32[]{:S(2)}, u32[]{:S(2)}) collective-permute-start(f32[128,128]{1,0:T(8,128)} %bitcast.15), channel_id=1, source_target_pairs={{0,24},{4,28},{8,16},{12,20},{16,8},{20,12},{24,0},{28,4},{1,25},{... | collective-permute-start | bytes 196616 | tf_op jit(solution)/shard_map/ppermute | solution.py:200
  4.7 0.5 %collective-permute-start.1 = (f32[128,128]{1,0:T(8,128)}, f32[128,128]{1,0:T(8,128)S(1)}, u32[]{:S(2)}, u32[]{:S(2)}) collective-permute-start(f32[128,128]{1,0:T(8,128)} %bitcast.16), channel_id=1, source_target_pairs={{0,16},{4,20},{8,24},{12,28},{16,0},{20,4},{24,8},{28,12},{1,17},{... | collective-permute-start | bytes 196616 | tf_op jit(solution)/shard_map/ppermute | solution.py:200
  5.2 0.1 collective-permute-start
  5.3 0.0 copy-start.6
  5.3 0.0 copy-start.7
  5.3 0.0 copy-start.8
  5.4 1.8 %collective-permute-done.2.refs_3_ = f32[128,128]{1,0:T(8,128)S(1)} collective-permute-done((f32[128,128]{1,0:T(8,128)}, f32[128,128]{1,0:T(8,128)S(1)}, u32[]{:S(2)}, u32[]{:S(2)}) %collective-permute-start.2) | collective-permute-done | bytes 65568 | tf_op jit(solution)/shard_map/ppermute | solution.py:200
  7.1 2.0 %collective-permute-done.1.refs_2_ = f32[128,128]{1,0:T(8,128)S(1)} collective-permute-done((f32[128,128]{1,0:T(8,128)}, f32[128,128]{1,0:T(8,128)S(1)}, u32[]{:S(2)}, u32[]{:S(2)}) %collective-permute-start.1) | collective-permute-done | bytes 65568 | tf_op jit(solution)/shard_map/ppermute | solution.py:200
  9.1 0.5 %collective-permute-done.refs_1_ = f32[128,128]{1,0:T(8,128)S(1)} collective-permute-done((f32[128,128]{1,0:T(8,128)}, f32[128,128]{1,0:T(8,128)S(1)}, u32[]{:S(2)}, u32[]{:S(2)}) %collective-permute-start) | collective-permute-done | bytes 65568 | tf_op jit(solution)/shard_map/ppermute | solution.py:200
  9.7 0.1 collective-permute-start.3
  9.8 3.7 %collective-permute-start.9 = (f32[128,128]{1,0:T(8,128)S(1)}, f32[128,128]{1,0:T(8,128)S(1)}, u32[]{:S(2)}, u32[]{:S(2)}) collective-permute-start(f32[128,128]{1,0:T(8,128)S(1)} %bitcast.19), channel_id=1, source_target_pairs={{0,3},{1,2},{2,1},{3,0},{4,7},{5,6},{6,5},{7,4},{8,11},{9,10},{10,... | collective-permute-start | bytes 196616 | tf_op jit(solution)/shard_map/ppermute | solution.py:200
  13.4 0.0 collective-permute-start.8
  13.4 0.8 %collective-permute-start.7 = (f32[128,128]{1,0:T(8,128)S(1)}, f32[128,128]{1,0:T(8,128)S(1)}, u32[]{:S(2)}, u32[]{:S(2)}) collective-permute-start(f32[128,128]{1,0:T(8,128)S(1)} %bitcast.21), channel_id=1, source_target_pairs={{0,1},{1,0},{2,3},{3,2},{4,5},{5,4},{6,7},{7,6},{8,9},{9,8},{10,11... | collective-permute-start | bytes 196616 | tf_op jit(solution)/shard_map/ppermute | solution.py:200
  14.2 0.6 %shard_map.113.start_ref = s32[2,256]{1,0:T(2,128)S(4)} custom-call(s32[2,256]{1,0:T(2,128)S(1)} %bitcast.23, s32[1,256]{1,0:T(1,128)S(1)} %bitcast.24), custom_call_target="tpu_custom_call" | custom-call | tf_op jit(solution)/shard_map/pallas_call | solution.py:223
  14.8 0.0 collective-permute-done.3.odd_ref
  14.8 2.5 %shard_map.116.refs_1_ = f32[1,256]{1,0:T(1,128)S(1)} custom-call(s32[2,256]{1,0:T(2,128)S(4)} %shard_map.113.start_ref, bf16[256,2,8,8,128]{4,3,2,1,0:T(8,128)(2,1)S(1)} %bitcast.13, f32[8,128]{1,0:T(8,128)S(1)} %shard_map.114.ones_ref, f32[4,128,128]{2,1,0:T(8,128)S(1)} %shard_map.115.even_ref, f32[4,128,128]{2,1,0:T(8,128)S(1)} %collective-permute-done.3.odd_ref), custom_call_target="tpu_custom_call" | custom-call | tf_op jit(solution)/shard_map/pallas_call | solution.py:231
  17.3 3.6 %collective-permute-start.6 = (f32[1,256]{1,0:T(1,128)S(1)}, f32[1,256]{1,0:T(1,128)S(1)}, u32[]{:S(2)}, u32[]{:S(2)}) collective-permute-start(f32[1,256]{1,0:T(1,128)S(1)} %shard_map.116.refs_1_), channel_id=1, source_target_pairs={{0,3},{1,2},{2,1},{3,0},{4,7},{5,6},{6,5},{7,4},{8,11},{9,10},{10,... | collective-permute-start | bytes 3080 | tf_op jit(solution)/shard_map/ppermute | solution.py:200
  20.9 0.0 collective-permute-start.5
  20.9 0.0 collective-permute-done.9.refs_3_
  20.9 0.8 %collective-permute-start.4 = (f32[1,256]{1,0:T(1,128)S(1)}, f32[1,256]{1,0:T(1,128)S(1)}, u32[]{:S(2)}, u32[]{:S(2)}) collective-permute-start(f32[1,256]{1,0:T(1,128)S(1)} %shard_map.116.refs_1_), channel_id=1, source_target_pairs={{0,1},{1,0},{2,3},{3,2},{4,5},{5,4},{6,7},{7,6},{8,9},{9,8},{10,11... | collective-permute-start | bytes 3080 | tf_op jit(solution)/shard_map/ppermute | solution.py:200
  21.7 0.0 collective-permute-done.8.refs_2_
  21.7 0.0 collective-permute-done.7.refs_1_
  21.8 1.0 %shard_map.117.refs_8_ = f32[1024,128]{1,0:T(8,128)S(1)} custom-call(f32[128,128]{1,0:T(8,128)S(1)} %bitcast.22, f32[128,128]{1,0:T(8,128)S(1)} %collective-permute-done.7.refs_1_, f32[128,128]{1,0:T(8,128)S(1)} %collective-permute-done.8.refs_2_, f32[128,128]{1,0:T(8,128)S(1)} %collective-permute-done.9.refs_3_, f32[128,512]{1,0:T(8,128)S(1)} %copy-done, ...), custom_call_target="tpu_custom_call" | custom-call | tf_op jit(solution)/shard_map/pallas_call | solution.py:243
  22.8 0.0 collective-permute-done.6.refs_4_
  22.8 2.6 %collective-permute-done.5.refs_3_ = f32[1,256]{1,0:T(1,128)S(1)} collective-permute-done((f32[1,256]{1,0:T(1,128)S(1)}, f32[1,256]{1,0:T(1,128)S(1)}, u32[]{:S(2)}, u32[]{:S(2)}) %collective-permute-start.5) | collective-permute-done | bytes 1056 | tf_op jit(solution)/shard_map/ppermute | solution.py:200
  25.4 0.0 collective-permute-done.4.refs_2_
  25.4 2.5 %shard_map.118 = (f32[128,128]{1,0:T(8,128)S(1)}, f32[128,128]{1,0:T(8,128)S(1)}, f32[128,128]{1,0:T(8,128)S(1)}, f32[128,128]{1,0:T(8,128)S(1)}, f32[128,128]{1...) custom-call(s32[2,256]{1,0:T(2,128)S(4)} %shard_map.113.start_ref, ...), custom_call_target="tpu_custom_call" | custom-call | tf_op jit(solution)/shard_map/pallas_call | solution.py:251
  28.0 0.1 collective-permute-start.10
  28.0 0.5 %collective-permute-start.12 = (f32[128,128]{1,0:T(8,128)S(1)}, f32[128,128]{1,0:T(8,128)S(1)}, u32[]{:S(2)}, u32[]{:S(2)}) collective-permute-start(f32[128,128]{1,0:T(8,128)S(1)} %get-tuple-element.14), channel_id=1, source_target_pairs={{0,4},{4,0},{8,12},{12,8},{16,20},{20,16},{24,28},{28,24},{1,5},{5... | collective-permute-start | bytes 196616 | tf_op jit(solution)/shard_map/ppermute | solution.py:200
  28.5 0.1 collective-permute-start.14
  28.6 0.4 %collective-permute-start.16 = (f32[128,128]{1,0:T(8,128)S(1)}, f32[128,128]{1,0:T(8,128)S(1)}, u32[]{:S(2)}, u32[]{:S(2)}) collective-permute-start(f32[128,128]{1,0:T(8,128)S(1)} %get-tuple-element.18), channel_id=1, source_target_pairs={{0,4},{4,0},{8,12},{12,8},{16,20},{20,16},{24,28},{28,24},{1,5},{5... | collective-permute-start | bytes 196616 | tf_op jit(solution)/shard_map/ppermute | solution.py:200
  29.1 0.2 collective-permute-done.10
  29.3 1.6 %collective-permute-start.11 = (f32[128,128]{1,0:T(8,128)S(1)}, f32[128,128]{1,0:T(8,128)S(1)}, u32[]{:S(2)}, u32[]{:S(2)}) collective-permute-start(f32[128,128]{1,0:T(8,128)S(1)} %add.21), channel_id=1, source_target_pairs={{0,24},{4,28},{8,16},{12,20},{16,8},{20,12},{24,0},{28,4},{1,25},{... | collective-permute-start | bytes 196616 | tf_op jit(solution)/shard_map/ppermute | solution.py:200
  30.9 0.0 collective-permute-done.12
  30.9 0.6 %collective-permute-start.13 = (f32[128,128]{1,0:T(8,128)S(1)}, f32[128,128]{1,0:T(8,128)S(1)}, u32[]{:S(2)}, u32[]{:S(2)}) collective-permute-start(f32[128,128]{1,0:T(8,128)S(1)} %add.22), channel_id=1, source_target_pairs={{0,16},{4,20},{8,24},{12,28},{16,0},{20,4},{24,8},{28,12},{1,17},{... | collective-permute-start | bytes 196616 | tf_op jit(solution)/shard_map/ppermute | solution.py:200
  31.5 0.0 collective-permute-done.14
  31.5 1.5 %collective-permute-start.15 = (f32[128,128]{1,0:T(8,128)S(1)}, f32[128,128]{1,0:T(8,128)S(1)}, u32[]{:S(2)}, u32[]{:S(2)}) collective-permute-start(f32[128,128]{1,0:T(8,128)S(1)} %add.24), channel_id=1, source_target_pairs={{0,8},{4,12},{8,0},{12,4},{16,24},{20,28},{24,16},{28,20},{1,9},{5... | collective-permute-start | bytes 196616 | tf_op jit(solution)/shard_map/ppermute | solution.py:200
  33.0 0.6 %slice.3 = f32[1,256]{1,0:T(1,128)} slice(f32[8,256]{1,0:T(8,128)S(1)} %get-tuple-element.19), slice={[0:1], [0:256]} | slice | bytes 2048 | tf_op jit(solution)/shard_map/slice | solution.py:267
  33.6 0.0 collective-permute-done.16
  33.6 0.9 %collective-permute-done.11 = f32[128,128]{1,0:T(8,128)S(1)} collective-permute-done((f32[128,128]{1,0:T(8,128)S(1)}, f32[128,128]{1,0:T(8,128)S(1)}, u32[]{:S(2)}, u32[]{:S(2)}) %collective-permute-start.11) | collective-permute-done | bytes 65568 | tf_op jit(solution)/shard_map/ppermute | solution.py:200
  34.5 1.3 %collective-permute-done.13 = f32[128,128]{1,0:T(8,128)S(1)} collective-permute-done((f32[128,128]{1,0:T(8,128)S(1)}, f32[128,128]{1,0:T(8,128)S(1)}, u32[]{:S(2)}, u32[]{:S(2)}) %collective-permute-start.13) | collective-permute-done | bytes 65568 | tf_op jit(solution)/shard_map/ppermute | solution.py:200
  35.8 0.1 collective-permute-done.15
  35.9 0.7 %add_add_fusion = f32[128,128]{1,0:T(8,128)} fusion(f32[128,128]{1,0:T(8,128)S(1)} %get-tuple-element.17, f32[128,128]{1,0:T(8,128)S(1)} %collective-permute-done.16, f32[128,128]{1,0:T(8,128)S(1)} %collective-permute-done.15, f32[128,128]{1,0:T(8,128)S(1)} %collective-permute-done.11, f32[128,128]{1,0:T(8,128)S(1)} %collective-permute-done.13), kind=kLoop, calls=%fused_computation | loop fusion | flops 65536 | bytes 393216 | tf_op jit(solution)/shard_map/add | solution.py:272
  (20 shorter events, 0.1 us)
Async XLA Ops:
  0.6 14.2 %slice-start = ((s8[8388608]{0:T(1024)(128)(4,1)}), s8[4194304]{0:T(1024)(128)(4,1)S(1)}, s32[]{:S(2)}) async-start(s8[8388608]{0:T(1024)(128)(4,1)} %bitcast.11), calls=%async_computation | async-start | bytes 8388608
  0.6 9.0 %copy-start.1 = (f32[64,2,128]{2,1,0:T(2,128)S(1)}, f32[64,2,128]{2,1,0:T(2,128)}, u32[]{:S(2)}) copy-start(f32[64,2,128]{2,1,0:T(2,128)} %param.10) | copy-start | bytes 196612
  0.7 13.6 %copy-start.4 = (s32[256,1,2]{0,2,1:T(2,128)S(1)}, s32[256,1,2]{0,2,1:T(2,128)}, u32[]{:S(2)}) copy-start(s32[256,1,2]{0,2,1:T(2,128)} %param.12) | copy-start | bytes 6148
  0.7 13.6 %copy-start.5 = (s32[256]{0:T(256)S(1)}, s32[256]{0:T(256)}, u32[]{:S(2)}) copy-start(s32[256]{0:T(256)} %param.13) | copy-start | bytes 3076
  0.7 14.2 %slice-start.1 = ((s8[8388608]{0:T(1024)(128)(4,1)}), s8[4194304]{0:T(1024)(128)(4,1)S(1)}, s32[]{:S(2)}) async-start(s8[8388608]{0:T(1024)(128)(4,1)} %bitcast.11), calls=%async_computation.1 | async-start | bytes 8388608
  0.7 6.4 %collective-permute-start.2 = (f32[128,128]{1,0:T(8,128)}, f32[128,128]{1,0:T(8,128)S(1)}, u32[]{:S(2)}, u32[]{:S(2)}) collective-permute-start(f32[128,128]{1,0:T(8,128)} %bitcast.15), channel_id=1, source_target_pairs={{0,24},{4,28},{8,16},{12,20},{16,8},{20,12},{24,0},{28,4},{1,25},{... | collective-permute-start | bytes 196616 | tf_op jit(solution)/shard_map/ppermute | solution.py:200
  4.7 4.5 %collective-permute-start.1 = (f32[128,128]{1,0:T(8,128)}, f32[128,128]{1,0:T(8,128)S(1)}, u32[]{:S(2)}, u32[]{:S(2)}) collective-permute-start(f32[128,128]{1,0:T(8,128)} %bitcast.16), channel_id=1, source_target_pairs={{0,16},{4,20},{8,24},{12,28},{16,0},{20,4},{24,8},{28,12},{1,17},{... | collective-permute-start | bytes 196616 | tf_op jit(solution)/shard_map/ppermute | solution.py:200
  5.2 4.5 %collective-permute-start = (f32[128,128]{1,0:T(8,128)}, f32[128,128]{1,0:T(8,128)S(1)}, u32[]{:S(2)}, u32[]{:S(2)}) collective-permute-start(f32[128,128]{1,0:T(8,128)} %bitcast.17), channel_id=1, source_target_pairs={{0,8},{4,12},{8,0},{12,4},{16,24},{20,28},{24,16},{28,20},{1,9},{5... | collective-permute-start | bytes 196616 | tf_op jit(solution)/shard_map/ppermute | solution.py:200
  5.3 16.4 %copy-start = (f32[128,512]{1,0:T(8,128)S(1)}, f32[128,512]{1,0:T(8,128)}, u32[]{:S(2)}) copy-start(f32[128,512]{1,0:T(8,128)} %refs_4_.1) | copy-start | bytes 786436
  5.3 16.4 %copy-start.2 = (f32[64,64]{1,0:T(8,128)S(1)}, f32[64,64]{1,0:T(8,128)}, u32[]{:S(2)}) copy-start(f32[64,64]{1,0:T(8,128)} %refs_5_.1) | copy-start | bytes 49156
  5.3 16.4 %copy-start.3 = (f32[16,16]{1,0:T(8,128)S(1)}, f32[16,16]{1,0:T(8,128)}, u32[]{:S(2)}) copy-start(f32[16,16]{1,0:T(8,128)} %refs_6_.1) | copy-start | bytes 3076
  5.3 20.1 %copy-start.6 = (f32[256]{0:T(256)S(1)}, f32[256]{0:T(256)}, u32[]{:S(2)}) copy-start(f32[256]{0:T(256)} %param.14) | copy-start | bytes 3076
  5.3 20.1 %copy-start.7 = (s32[256]{0:T(256)S(1)}, s32[256]{0:T(256)}, u32[]{:S(2)}) copy-start(s32[256]{0:T(256)} %param.15) | copy-start | bytes 3076
  5.3 20.1 %copy-start.8 = (f32[4]{0:T(128)S(1)}, f32[4]{0:T(128)}, u32[]{:S(2)}) copy-start(f32[4]{0:T(128)} %param.16) | copy-start | bytes 52
  9.7 5.1 %collective-permute-start.3 = (f32[4,128,128]{2,1,0:T(8,128)S(1)}, f32[4,128,128]{2,1,0:T(8,128)S(1)}, u32[]{:S(2)}, u32[]{:S(2)}) collective-permute-start(f32[4,128,128]{2,1,0:T(8,128)S(1)} %shard_map.115.even_ref), channel_id=1, source_target_pairs={{0,4},{4,0},{8,12},{12,8},{16,20},{20,16},{24,28},{28,24},{1,5},{5... | collective-permute-start | bytes 786440 | tf_op jit(solution)/shard_map/ppermute | solution.py:200
  9.8 11.2 %collective-permute-start.9 = (f32[128,128]{1,0:T(8,128)S(1)}, f32[128,128]{1,0:T(8,128)S(1)}, u32[]{:S(2)}, u32[]{:S(2)}) collective-permute-start(f32[128,128]{1,0:T(8,128)S(1)} %bitcast.19), channel_id=1, source_target_pairs={{0,3},{1,2},{2,1},{3,0},{4,7},{5,6},{6,5},{7,4},{8,11},{9,10},{10,... | collective-permute-start | bytes 196616 | tf_op jit(solution)/shard_map/ppermute | solution.py:200
  13.4 8.3 %collective-permute-start.8 = (f32[128,128]{1,0:T(8,128)S(1)}, f32[128,128]{1,0:T(8,128)S(1)}, u32[]{:S(2)}, u32[]{:S(2)}) collective-permute-start(f32[128,128]{1,0:T(8,128)S(1)} %bitcast.20), channel_id=1, source_target_pairs={{0,2},{1,3},{2,0},{3,1},{4,6},{5,7},{6,4},{7,5},{8,10},{9,11},{10,... | collective-permute-start | bytes 196616 | tf_op jit(solution)/shard_map/ppermute | solution.py:200
  13.4 8.3 %collective-permute-start.7 = (f32[128,128]{1,0:T(8,128)S(1)}, f32[128,128]{1,0:T(8,128)S(1)}, u32[]{:S(2)}, u32[]{:S(2)}) collective-permute-start(f32[128,128]{1,0:T(8,128)S(1)} %bitcast.21), channel_id=1, source_target_pairs={{0,1},{1,0},{2,3},{3,2},{4,5},{5,4},{6,7},{7,6},{8,9},{9,8},{10,11... | collective-permute-start | bytes 196616 | tf_op jit(solution)/shard_map/ppermute | solution.py:200
  17.3 5.5 %collective-permute-start.6 = (f32[1,256]{1,0:T(1,128)S(1)}, f32[1,256]{1,0:T(1,128)S(1)}, u32[]{:S(2)}, u32[]{:S(2)}) collective-permute-start(f32[1,256]{1,0:T(1,128)S(1)} %shard_map.116.refs_1_), channel_id=1, source_target_pairs={{0,3},{1,2},{2,1},{3,0},{4,7},{5,6},{6,5},{7,4},{8,11},{9,10},{10,... | collective-permute-start | bytes 3080 | tf_op jit(solution)/shard_map/ppermute | solution.py:200
  20.9 4.5 %collective-permute-start.5 = (f32[1,256]{1,0:T(1,128)S(1)}, f32[1,256]{1,0:T(1,128)S(1)}, u32[]{:S(2)}, u32[]{:S(2)}) collective-permute-start(f32[1,256]{1,0:T(1,128)S(1)} %shard_map.116.refs_1_), channel_id=1, source_target_pairs={{0,2},{1,3},{2,0},{3,1},{4,6},{5,7},{6,4},{7,5},{8,10},{9,11},{10,... | collective-permute-start | bytes 3080 | tf_op jit(solution)/shard_map/ppermute | solution.py:200
  20.9 4.5 %collective-permute-start.4 = (f32[1,256]{1,0:T(1,128)S(1)}, f32[1,256]{1,0:T(1,128)S(1)}, u32[]{:S(2)}, u32[]{:S(2)}) collective-permute-start(f32[1,256]{1,0:T(1,128)S(1)} %shard_map.116.refs_1_), channel_id=1, source_target_pairs={{0,1},{1,0},{2,3},{3,2},{4,5},{5,4},{6,7},{7,6},{8,9},{9,8},{10,11... | collective-permute-start | bytes 3080 | tf_op jit(solution)/shard_map/ppermute | solution.py:200
  28.0 1.3 %collective-permute-start.10 = (f32[128,128]{1,0:T(8,128)S(1)}, f32[128,128]{1,0:T(8,128)S(1)}, u32[]{:S(2)}, u32[]{:S(2)}) collective-permute-start(f32[128,128]{1,0:T(8,128)S(1)} %get-tuple-element.12), channel_id=1, source_target_pairs={{0,4},{4,0},{8,12},{12,8},{16,20},{20,16},{24,28},{28,24},{1,5},{5... | collective-permute-start | bytes 196616 | tf_op jit(solution)/shard_map/ppermute | solution.py:200
  28.0 2.8 %collective-permute-start.12 = (f32[128,128]{1,0:T(8,128)S(1)}, f32[128,128]{1,0:T(8,128)S(1)}, u32[]{:S(2)}, u32[]{:S(2)}) collective-permute-start(f32[128,128]{1,0:T(8,128)S(1)} %get-tuple-element.14), channel_id=1, source_target_pairs={{0,4},{4,0},{8,12},{12,8},{16,20},{20,16},{24,28},{28,24},{1,5},{5... | collective-permute-start | bytes 196616 | tf_op jit(solution)/shard_map/ppermute | solution.py:200
  28.5 2.9 %collective-permute-start.14 = (f32[128,128]{1,0:T(8,128)S(1)}, f32[128,128]{1,0:T(8,128)S(1)}, u32[]{:S(2)}, u32[]{:S(2)}) collective-permute-start(f32[128,128]{1,0:T(8,128)S(1)} %get-tuple-element.16), channel_id=1, source_target_pairs={{0,4},{4,0},{8,12},{12,8},{16,20},{20,16},{24,28},{28,24},{1,5},{5... | collective-permute-start | bytes 196616 | tf_op jit(solution)/shard_map/ppermute | solution.py:200
  28.6 5.0 %collective-permute-start.16 = (f32[128,128]{1,0:T(8,128)S(1)}, f32[128,128]{1,0:T(8,128)S(1)}, u32[]{:S(2)}, u32[]{:S(2)}) collective-permute-start(f32[128,128]{1,0:T(8,128)S(1)} %get-tuple-element.18), channel_id=1, source_target_pairs={{0,4},{4,0},{8,12},{12,8},{16,20},{20,16},{24,28},{28,24},{1,5},{5... | collective-permute-start | bytes 196616 | tf_op jit(solution)/shard_map/ppermute | solution.py:200
  29.3 5.2 %collective-permute-start.11 = (f32[128,128]{1,0:T(8,128)S(1)}, f32[128,128]{1,0:T(8,128)S(1)}, u32[]{:S(2)}, u32[]{:S(2)}) collective-permute-start(f32[128,128]{1,0:T(8,128)S(1)} %add.21), channel_id=1, source_target_pairs={{0,24},{4,28},{8,16},{12,20},{16,8},{20,12},{24,0},{28,4},{1,25},{... | collective-permute-start | bytes 196616 | tf_op jit(solution)/shard_map/ppermute | solution.py:200
  30.9 5.0 %collective-permute-start.13 = (f32[128,128]{1,0:T(8,128)S(1)}, f32[128,128]{1,0:T(8,128)S(1)}, u32[]{:S(2)}, u32[]{:S(2)}) collective-permute-start(f32[128,128]{1,0:T(8,128)S(1)} %add.22), channel_id=1, source_target_pairs={{0,16},{4,20},{8,24},{12,28},{16,0},{20,4},{24,8},{28,12},{1,17},{... | collective-permute-start | bytes 196616 | tf_op jit(solution)/shard_map/ppermute | solution.py:200
  31.5 4.4 %collective-permute-start.15 = (f32[128,128]{1,0:T(8,128)S(1)}, f32[128,128]{1,0:T(8,128)S(1)}, u32[]{:S(2)}, u32[]{:S(2)}) collective-permute-start(f32[128,128]{1,0:T(8,128)S(1)} %add.24), channel_id=1, source_target_pairs={{0,8},{4,12},{8,0},{12,4},{16,24},{20,28},{24,16},{28,20},{1,9},{5... | collective-permute-start | bytes 196616 | tf_op jit(solution)/shard_map/ppermute | solution.py:200

commit v4 on v3

--- a/solution.py
+++ b/solution.py
@@ -44,7 +44,7 @@
         refs[-1][index] = block[...]
 
 
-def forward_kernel(dims, start_ref, foot_ref, ones_ref, even_ref, odd_ref, *refs):
+def forward_kernel(dims, start_ref, foot_ref, even_ref, odd_ref, *refs):
     periods, tiles_y, tile_rows, lat_dev, receptors, slots, window = dims
     out_ref, table, sums = refs
     lanes = table.shape[-1]
@@ -77,8 +77,7 @@
     rows = sums[pl.ds(0, receptors, stride=tile_rows), :]
     for row in range(1, tile_rows):
         rows = rows + sums[pl.ds(row, receptors, stride=tile_rows), :]
-    flat = dot(ones_ref[...], rows, ((1,), (1,)))
-    out_ref[...] = flat[0:1, :]
+    out_ref[...] = jnp.sum(jnp.transpose(rows), axis=0, keepdims=True)
 
 
 def prior_kernel(dims, n_tile, *refs):
@@ -231,14 +230,14 @@
     partial_pred = pl.pallas_call(
         functools.partial(forward_kernel, dims),
         out_shape=line_shape,
-        in_specs=[smem] + [vmem] * 4,
+        in_specs=[smem] + [vmem] * 3,
         out_specs=vmem,
         scratch_shapes=[
             table_shape,
             pltpu.VMEM((receptors * tile_rows, lon_dev), jnp.float32),
         ],
         compiler_params=params,
-    )(starts, foot, ones, even, odd)
+    )(starts, foot, even, odd)
     preds = [partial_pred] + [swap(partial_pred, "tile", d) for d in range(1, n_tile)]
     prior = pl.pallas_call(
         functools.partial(prior_kernel, dims, n_tile),

time: 36.7 us -> 36.6 us (level)
  no operation moved by 1% of the time
where the time goes in v4:
time: 36.6 us; the launch traced here: 36.5 us
  starting transfers between devices  18.4 us (50%)
  waiting for transfers between devices  9.45 us (26%)
  Pallas kernels  6.52 us (18%)
  between operations  0.84 us (2%)
  other arithmetic  0.68 us (2%)
  local copies, waits for them, and re-layouts  0.61 us (2%)
    ppermute x17, starting transfers between devices, swap(): return lax.ppermute(value, axis, [(i, i ^ dist) for i in range(size)])  18.4 us
    ppermute x17, waiting for transfers between devices, swap(): return lax.ppermute(value, axis, [(i, i ^ dist) for i in range(size)])  9.45 us
    pallas_call x1, Pallas kernels, shards(): pl.pallas_call(functools.partial(adjoint_kernel, dims, n_tile), out_shape...  2.53 us
    pallas_call x1, Pallas kernels, shards(): pl.pallas_call(functools.partial(forward_kernel, dims), out_shape=line_sh...  2.36 us
    pallas_call x1, Pallas kernels, shards(): pl.pallas_call(functools.partial(prior_kernel, dims, n_tile), out_shape=p...  1.03 us
  transfers between devices with their start and end apart: 17, of which 8 were waited for; matrix products, arithmetic and copies ran while one was open for 2% of the time, Pallas kernels for 11%

profile of v4, /device:TPU:0, one launch (start us, length us, event | category | flops | bytes accessed | tf_op | source)
XLA Modules:
  0.0 36.5 jit_solution(12974253074915717052)
XLA Ops:
  0.6 0.0 slice-start
  0.6 0.0 copy-start.1
  0.7 0.0 copy-start.4
  0.7 0.0 copy-start.5
  0.7 0.0 slice-start.1
  0.7 4.0 %collective-permute-start.2 = (f32[128,128]{1,0:T(8,128)}, f32[128,128]{1,0:T(8,128)S(1)}, u32[]{:S(2)}, u32[]{:S(2)}) collective-permute-start(f32[128,128]{1,0:T(8,128)} %bitcast.15), channel_id=1, source_target_pairs={{0,24},{4,28},{8,16},{12,20},{16,8},{20,12},{24,0},{28,4},{1,25},{... | collective-permute-start | bytes 196616 | tf_op jit(solution)/shard_map/ppermute | solution.py:199
  4.7 0.5 %collective-permute-start.1 = (f32[128,128]{1,0:T(8,128)}, f32[128,128]{1,0:T(8,128)S(1)}, u32[]{:S(2)}, u32[]{:S(2)}) collective-permute-start(f32[128,128]{1,0:T(8,128)} %bitcast.16), channel_id=1, source_target_pairs={{0,16},{4,20},{8,24},{12,28},{16,0},{20,4},{24,8},{28,12},{1,17},{... | collective-permute-start | bytes 196616 | tf_op jit(solution)/shard_map/ppermute | solution.py:199
  5.2 0.1 collective-permute-start
  5.3 0.0 copy-start.6
  5.3 0.0 copy-start.7
  5.3 0.0 copy-start.8
  5.4 1.8 %collective-permute-done.2.refs_3_ = f32[128,128]{1,0:T(8,128)S(1)} collective-permute-done((f32[128,128]{1,0:T(8,128)}, f32[128,128]{1,0:T(8,128)S(1)}, u32[]{:S(2)}, u32[]{:S(2)}) %collective-permute-start.2) | collective-permute-done | bytes 65568 | tf_op jit(solution)/shard_map/ppermute | solution.py:199
  7.1 2.0 %collective-permute-done.1.refs_2_ = f32[128,128]{1,0:T(8,128)S(1)} collective-permute-done((f32[128,128]{1,0:T(8,128)}, f32[128,128]{1,0:T(8,128)S(1)}, u32[]{:S(2)}, u32[]{:S(2)}) %collective-permute-start.1) | collective-permute-done | bytes 65568 | tf_op jit(solution)/shard_map/ppermute | solution.py:199
  9.1 0.5 %collective-permute-done.refs_1_ = f32[128,128]{1,0:T(8,128)S(1)} collective-permute-done((f32[128,128]{1,0:T(8,128)}, f32[128,128]{1,0:T(8,128)S(1)}, u32[]{:S(2)}, u32[]{:S(2)}) %collective-permute-start) | collective-permute-done | bytes 65568 | tf_op jit(solution)/shard_map/ppermute | solution.py:199
  9.7 0.1 collective-permute-start.3
  9.8 3.7 %collective-permute-start.9 = (f32[128,128]{1,0:T(8,128)S(1)}, f32[128,128]{1,0:T(8,128)S(1)}, u32[]{:S(2)}, u32[]{:S(2)}) collective-permute-start(f32[128,128]{1,0:T(8,128)S(1)} %bitcast.19), channel_id=1, source_target_pairs={{0,3},{1,2},{2,1},{3,0},{4,7},{5,6},{6,5},{7,4},{8,11},{9,10},{10,... | collective-permute-start | bytes 196616 | tf_op jit(solution)/shard_map/ppermute | solution.py:199
  13.4 0.0 collective-permute-start.8
  13.4 0.8 %collective-permute-start.7 = (f32[128,128]{1,0:T(8,128)S(1)}, f32[128,128]{1,0:T(8,128)S(1)}, u32[]{:S(2)}, u32[]{:S(2)}) collective-permute-start(f32[128,128]{1,0:T(8,128)S(1)} %bitcast.21), channel_id=1, source_target_pairs={{0,1},{1,0},{2,3},{3,2},{4,5},{5,4},{6,7},{7,6},{8,9},{9,8},{10,11... | collective-permute-start | bytes 196616 | tf_op jit(solution)/shard_map/ppermute | solution.py:199
  14.2 0.6 %shard_map.113.start_ref = s32[2,256]{1,0:T(2,128)S(4)} custom-call(s32[2,256]{1,0:T(2,128)S(1)} %bitcast.23, s32[1,256]{1,0:T(1,128)S(1)} %bitcast.24), custom_call_target="tpu_custom_call" | custom-call | tf_op jit(solution)/shard_map/pallas_call | solution.py:222
  14.8 0.0 collective-permute-done.3.odd_ref
  14.8 2.4 %shard_map.116.refs_1_ = f32[1,256]{1,0:T(1,128)S(1)} custom-call(s32[2,256]{1,0:T(2,128)S(4)} %shard_map.113.start_ref, bf16[256,2,8,8,128]{4,3,2,1,0:T(8,128)(2,1)S(1)} %bitcast.13, f32[4,128,128]{2,1,0:T(8,128)S(1)} %shard_map.115.even_ref, f32[4,128,128]{2,1,0:T(8,128)S(1)} %collective-permute-done.3.odd_ref), custom_call_target="tpu_custom_call" | custom-call | tf_op jit(solution)/shard_map/pallas_call | solution.py:230
  17.2 3.7 %collective-permute-start.6 = (f32[1,256]{1,0:T(1,128)S(1)}, f32[1,256]{1,0:T(1,128)S(1)}, u32[]{:S(2)}, u32[]{:S(2)}) collective-permute-start(f32[1,256]{1,0:T(1,128)S(1)} %shard_map.116.refs_1_), channel_id=1, source_target_pairs={{0,3},{1,2},{2,1},{3,0},{4,7},{5,6},{6,5},{7,4},{8,11},{9,10},{10,... | collective-permute-start | bytes 3080 | tf_op jit(solution)/shard_map/ppermute | solution.py:199
  20.9 0.0 collective-permute-start.5
  20.9 0.0 collective-permute-done.9.refs_3_
  20.9 0.8 %collective-permute-start.4 = (f32[1,256]{1,0:T(1,128)S(1)}, f32[1,256]{1,0:T(1,128)S(1)}, u32[]{:S(2)}, u32[]{:S(2)}) collective-permute-start(f32[1,256]{1,0:T(1,128)S(1)} %shard_map.116.refs_1_), channel_id=1, source_target_pairs={{0,1},{1,0},{2,3},{3,2},{4,5},{5,4},{6,7},{7,6},{8,9},{9,8},{10,11... | collective-permute-start | bytes 3080 | tf_op jit(solution)/shard_map/ppermute | solution.py:199
  21.7 0.0 collective-permute-done.8.refs_2_
  21.7 0.0 collective-permute-done.7.refs_1_
  21.7 1.0 %shard_map.117.refs_8_ = f32[1024,128]{1,0:T(8,128)S(1)} custom-call(f32[128,128]{1,0:T(8,128)S(1)} %bitcast.22, f32[128,128]{1,0:T(8,128)S(1)} %collective-permute-done.7.refs_1_, f32[128,128]{1,0:T(8,128)S(1)} %collective-permute-done.8.refs_2_, f32[128,128]{1,0:T(8,128)S(1)} %collective-permute-done.9.refs_3_, f32[128,512]{1,0:T(8,128)S(1)} %copy-done, ...), custom_call_target="tpu_custom_call" | custom-call | tf_op jit(solution)/shard_map/pallas_call | solution.py:242
  22.7 0.0 collective-permute-done.6.refs_4_
  22.7 2.6 %collective-permute-done.5.refs_3_ = f32[1,256]{1,0:T(1,128)S(1)} collective-permute-done((f32[1,256]{1,0:T(1,128)S(1)}, f32[1,256]{1,0:T(1,128)S(1)}, u32[]{:S(2)}, u32[]{:S(2)}) %collective-permute-start.5) | collective-permute-done | bytes 1056 | tf_op jit(solution)/shard_map/ppermute | solution.py:199
  25.3 0.0 collective-permute-done.4.refs_2_
  25.4 2.5 %shard_map.118 = (f32[128,128]{1,0:T(8,128)S(1)}, f32[128,128]{1,0:T(8,128)S(1)}, f32[128,128]{1,0:T(8,128)S(1)}, f32[128,128]{1,0:T(8,128)S(1)}, f32[128,128]{1...) custom-call(s32[2,256]{1,0:T(2,128)S(4)} %shard_map.113.start_ref, ...), custom_call_target="tpu_custom_call" | custom-call | tf_op jit(solution)/shard_map/pallas_call | solution.py:250
  27.9 0.1 collective-permute-start.10
  28.0 0.5 %collective-permute-start.12 = (f32[128,128]{1,0:T(8,128)S(1)}, f32[128,128]{1,0:T(8,128)S(1)}, u32[]{:S(2)}, u32[]{:S(2)}) collective-permute-start(f32[128,128]{1,0:T(8,128)S(1)} %get-tuple-element.14), channel_id=1, source_target_pairs={{0,4},{4,0},{8,12},{12,8},{16,20},{20,16},{24,28},{28,24},{1,5},{5... | collective-permute-start | bytes 196616 | tf_op jit(solution)/shard_map/ppermute | solution.py:199
  28.5 0.1 collective-permute-start.14
  28.6 0.4 %collective-permute-start.16 = (f32[128,128]{1,0:T(8,128)S(1)}, f32[128,128]{1,0:T(8,128)S(1)}, u32[]{:S(2)}, u32[]{:S(2)}) collective-permute-start(f32[128,128]{1,0:T(8,128)S(1)} %get-tuple-element.18), channel_id=1, source_target_pairs={{0,4},{4,0},{8,12},{12,8},{16,20},{20,16},{24,28},{28,24},{1,5},{5... | collective-permute-start | bytes 196616 | tf_op jit(solution)/shard_map/ppermute | solution.py:199
  29.0 0.2 collective-permute-done.10
  29.2 1.6 %collective-permute-start.11 = (f32[128,128]{1,0:T(8,128)S(1)}, f32[128,128]{1,0:T(8,128)S(1)}, u32[]{:S(2)}, u32[]{:S(2)}) collective-permute-start(f32[128,128]{1,0:T(8,128)S(1)} %add.21), channel_id=1, source_target_pairs={{0,24},{4,28},{8,16},{12,20},{16,8},{20,12},{24,0},{28,4},{1,25},{... | collective-permute-start | bytes 196616 | tf_op jit(solution)/shard_map/ppermute | solution.py:199
  30.8 0.0 collective-permute-done.12
  30.8 0.6 %collective-permute-start.13 = (f32[128,128]{1,0:T(8,128)S(1)}, f32[128,128]{1,0:T(8,128)S(1)}, u32[]{:S(2)}, u32[]{:S(2)}) collective-permute-start(f32[128,128]{1,0:T(8,128)S(1)} %add.22), channel_id=1, source_target_pairs={{0,16},{4,20},{8,24},{12,28},{16,0},{20,4},{24,8},{28,12},{1,17},{... | collective-permute-start | bytes 196616 | tf_op jit(solution)/shard_map/ppermute | solution.py:199
  31.4 0.0 collective-permute-done.14
  31.4 1.5 %collective-permute-start.15 = (f32[128,128]{1,0:T(8,128)S(1)}, f32[128,128]{1,0:T(8,128)S(1)}, u32[]{:S(2)}, u32[]{:S(2)}) collective-permute-start(f32[128,128]{1,0:T(8,128)S(1)} %add.24), channel_id=1, source_target_pairs={{0,8},{4,12},{8,0},{12,4},{16,24},{20,28},{24,16},{28,20},{1,9},{5... | collective-permute-start | bytes 196616 | tf_op jit(solution)/shard_map/ppermute | solution.py:199
  33.0 0.6 %slice.3 = f32[1,256]{1,0:T(1,128)} slice(f32[8,256]{1,0:T(8,128)S(1)} %get-tuple-element.19), slice={[0:1], [0:256]} | slice | bytes 2048 | tf_op jit(solution)/shard_map/slice | solution.py:266
  33.5 0.0 collective-permute-done.16
  33.5 0.9 %collective-permute-done.11 = f32[128,128]{1,0:T(8,128)S(1)} collective-permute-done((f32[128,128]{1,0:T(8,128)S(1)}, f32[128,128]{1,0:T(8,128)S(1)}, u32[]{:S(2)}, u32[]{:S(2)}) %collective-permute-start.11) | collective-permute-done | bytes 65568 | tf_op jit(solution)/shard_map/ppermute | solution.py:199
  34.5 1.3 %collective-permute-done.13 = f32[128,128]{1,0:T(8,128)S(1)} collective-permute-done((f32[128,128]{1,0:T(8,128)S(1)}, f32[128,128]{1,0:T(8,128)S(1)}, u32[]{:S(2)}, u32[]{:S(2)}) %collective-permute-start.13) | collective-permute-done | bytes 65568 | tf_op jit(solution)/shard_map/ppermute | solution.py:199
  35.8 0.1 collective-permute-done.15
  35.8 0.7 %add_add_fusion = f32[128,128]{1,0:T(8,128)} fusion(f32[128,128]{1,0:T(8,128)S(1)} %get-tuple-element.17, f32[128,128]{1,0:T(8,128)S(1)} %collective-permute-done.16, f32[128,128]{1,0:T(8,128)S(1)} %collective-permute-done.15, f32[128,128]{1,0:T(8,128)S(1)} %collective-permute-done.11, f32[128,128]{1,0:T(8,128)S(1)} %collective-permute-done.13), kind=kLoop, calls=%fused_computation | loop fusion | flops 65536 | bytes 393216 | tf_op jit(solution)/shard_map/add | solution.py:271
  (20 shorter events, 0.1 us)
Async XLA Ops:
  0.6 14.2 %slice-start = ((s8[8388608]{0:T(1024)(128)(4,1)}), s8[4194304]{0:T(1024)(128)(4,1)S(1)}, s32[]{:S(2)}) async-start(s8[8388608]{0:T(1024)(128)(4,1)} %bitcast.11), calls=%async_computation | async-start | bytes 8388608
  0.6 9.0 %copy-start.1 = (f32[64,2,128]{2,1,0:T(2,128)S(1)}, f32[64,2,128]{2,1,0:T(2,128)}, u32[]{:S(2)}) copy-start(f32[64,2,128]{2,1,0:T(2,128)} %param.10) | copy-start | bytes 196612
  0.7 13.6 %copy-start.4 = (s32[256,1,2]{0,2,1:T(2,128)S(1)}, s32[256,1,2]{0,2,1:T(2,128)}, u32[]{:S(2)}) copy-start(s32[256,1,2]{0,2,1:T(2,128)} %param.12) | copy-start | bytes 6148
  0.7 13.6 %copy-start.5 = (s32[256]{0:T(256)S(1)}, s32[256]{0:T(256)}, u32[]{:S(2)}) copy-start(s32[256]{0:T(256)} %param.13) | copy-start | bytes 3076
  0.7 14.2 %slice-start.1 = ((s8[8388608]{0:T(1024)(128)(4,1)}), s8[4194304]{0:T(1024)(128)(4,1)S(1)}, s32[]{:S(2)}) async-start(s8[8388608]{0:T(1024)(128)(4,1)} %bitcast.11), calls=%async_computation.1 | async-start | bytes 8388608
  0.7 6.4 %collective-permute-start.2 = (f32[128,128]{1,0:T(8,128)}, f32[128,128]{1,0:T(8,128)S(1)}, u32[]{:S(2)}, u32[]{:S(2)}) collective-permute-start(f32[128,128]{1,0:T(8,128)} %bitcast.15), channel_id=1, source_target_pairs={{0,24},{4,28},{8,16},{12,20},{16,8},{20,12},{24,0},{28,4},{1,25},{... | collective-permute-start | bytes 196616 | tf_op jit(solution)/shard_map/ppermute | solution.py:199
  4.7 4.5 %collective-permute-start.1 = (f32[128,128]{1,0:T(8,128)}, f32[128,128]{1,0:T(8,128)S(1)}, u32[]{:S(2)}, u32[]{:S(2)}) collective-permute-start(f32[128,128]{1,0:T(8,128)} %bitcast.16), channel_id=1, source_target_pairs={{0,16},{4,20},{8,24},{12,28},{16,0},{20,4},{24,8},{28,12},{1,17},{... | collective-permute-start | bytes 196616 | tf_op jit(solution)/shard_map/ppermute | solution.py:199
  5.2 4.5 %collective-permute-start = (f32[128,128]{1,0:T(8,128)}, f32[128,128]{1,0:T(8,128)S(1)}, u32[]{:S(2)}, u32[]{:S(2)}) collective-permute-start(f32[128,128]{1,0:T(8,128)} %bitcast.17), channel_id=1, source_target_pairs={{0,8},{4,12},{8,0},{12,4},{16,24},{20,28},{24,16},{28,20},{1,9},{5... | collective-permute-start | bytes 196616 | tf_op jit(solution)/shard_map/ppermute | solution.py:199
  5.3 16.4 %copy-start = (f32[128,512]{1,0:T(8,128)S(1)}, f32[128,512]{1,0:T(8,128)}, u32[]{:S(2)}) copy-start(f32[128,512]{1,0:T(8,128)} %refs_4_.1) | copy-start | bytes 786436
  5.3 16.4 %copy-start.2 = (f32[64,64]{1,0:T(8,128)S(1)}, f32[64,64]{1,0:T(8,128)}, u32[]{:S(2)}) copy-start(f32[64,64]{1,0:T(8,128)} %refs_5_.1) | copy-start | bytes 49156
  5.3 16.4 %copy-start.3 = (f32[16,16]{1,0:T(8,128)S(1)}, f32[16,16]{1,0:T(8,128)}, u32[]{:S(2)}) copy-start(f32[16,16]{1,0:T(8,128)} %refs_6_.1) | copy-start | bytes 3076
  5.3 20.0 %copy-start.6 = (f32[256]{0:T(256)S(1)}, f32[256]{0:T(256)}, u32[]{:S(2)}) copy-start(f32[256]{0:T(256)} %param.14) | copy-start | bytes 3076
  5.3 20.0 %copy-start.7 = (s32[256]{0:T(256)S(1)}, s32[256]{0:T(256)}, u32[]{:S(2)}) copy-start(s32[256]{0:T(256)} %param.15) | copy-start | bytes 3076
  5.3 20.0 %copy-start.8 = (f32[4]{0:T(128)S(1)}, f32[4]{0:T(128)}, u32[]{:S(2)}) copy-start(f32[4]{0:T(128)} %param.16) | copy-start | bytes 52
  9.7 5.1 %collective-permute-start.3 = (f32[4,128,128]{2,1,0:T(8,128)S(1)}, f32[4,128,128]{2,1,0:T(8,128)S(1)}, u32[]{:S(2)}, u32[]{:S(2)}) collective-permute-start(f32[4,128,128]{2,1,0:T(8,128)S(1)} %shard_map.115.even_ref), channel_id=1, source_target_pairs={{0,4},{4,0},{8,12},{12,8},{16,20},{20,16},{24,28},{28,24},{1,5},{5... | collective-permute-start | bytes 786440 | tf_op jit(solution)/shard_map/ppermute | solution.py:199
  9.8 11.1 %collective-permute-start.9 = (f32[128,128]{1,0:T(8,128)S(1)}, f32[128,128]{1,0:T(8,128)S(1)}, u32[]{:S(2)}, u32[]{:S(2)}) collective-permute-start(f32[128,128]{1,0:T(8,128)S(1)} %bitcast.19), channel_id=1, source_target_pairs={{0,3},{1,2},{2,1},{3,0},{4,7},{5,6},{6,5},{7,4},{8,11},{9,10},{10,... | collective-permute-start | bytes 196616 | tf_op jit(solution)/shard_map/ppermute | solution.py:199
  13.4 8.2 %collective-permute-start.8 = (f32[128,128]{1,0:T(8,128)S(1)}, f32[128,128]{1,0:T(8,128)S(1)}, u32[]{:S(2)}, u32[]{:S(2)}) collective-permute-start(f32[128,128]{1,0:T(8,128)S(1)} %bitcast.20), channel_id=1, source_target_pairs={{0,2},{1,3},{2,0},{3,1},{4,6},{5,7},{6,4},{7,5},{8,10},{9,11},{10,... | collective-permute-start | bytes 196616 | tf_op jit(solution)/shard_map/ppermute | solution.py:199
  13.4 8.2 %collective-permute-start.7 = (f32[128,128]{1,0:T(8,128)S(1)}, f32[128,128]{1,0:T(8,128)S(1)}, u32[]{:S(2)}, u32[]{:S(2)}) collective-permute-start(f32[128,128]{1,0:T(8,128)S(1)} %bitcast.21), channel_id=1, source_target_pairs={{0,1},{1,0},{2,3},{3,2},{4,5},{5,4},{6,7},{7,6},{8,9},{9,8},{10,11... | collective-permute-start | bytes 196616 | tf_op jit(solution)/shard_map/ppermute | solution.py:199
  17.2 5.5 %collective-permute-start.6 = (f32[1,256]{1,0:T(1,128)S(1)}, f32[1,256]{1,0:T(1,128)S(1)}, u32[]{:S(2)}, u32[]{:S(2)}) collective-permute-start(f32[1,256]{1,0:T(1,128)S(1)} %shard_map.116.refs_1_), channel_id=1, source_target_pairs={{0,3},{1,2},{2,1},{3,0},{4,7},{5,6},{6,5},{7,4},{8,11},{9,10},{10,... | collective-permute-start | bytes 3080 | tf_op jit(solution)/shard_map/ppermute | solution.py:199
  20.9 4.5 %collective-permute-start.5 = (f32[1,256]{1,0:T(1,128)S(1)}, f32[1,256]{1,0:T(1,128)S(1)}, u32[]{:S(2)}, u32[]{:S(2)}) collective-permute-start(f32[1,256]{1,0:T(1,128)S(1)} %shard_map.116.refs_1_), channel_id=1, source_target_pairs={{0,2},{1,3},{2,0},{3,1},{4,6},{5,7},{6,4},{7,5},{8,10},{9,11},{10,... | collective-permute-start | bytes 3080 | tf_op jit(solution)/shard_map/ppermute | solution.py:199
  20.9 4.5 %collective-permute-start.4 = (f32[1,256]{1,0:T(1,128)S(1)}, f32[1,256]{1,0:T(1,128)S(1)}, u32[]{:S(2)}, u32[]{:S(2)}) collective-permute-start(f32[1,256]{1,0:T(1,128)S(1)} %shard_map.116.refs_1_), channel_id=1, source_target_pairs={{0,1},{1,0},{2,3},{3,2},{4,5},{5,4},{6,7},{7,6},{8,9},{9,8},{10,11... | collective-permute-start | bytes 3080 | tf_op jit(solution)/shard_map/ppermute | solution.py:199
  27.9 1.3 %collective-permute-start.10 = (f32[128,128]{1,0:T(8,128)S(1)}, f32[128,128]{1,0:T(8,128)S(1)}, u32[]{:S(2)}, u32[]{:S(2)}) collective-permute-start(f32[128,128]{1,0:T(8,128)S(1)} %get-tuple-element.12), channel_id=1, source_target_pairs={{0,4},{4,0},{8,12},{12,8},{16,20},{20,16},{24,28},{28,24},{1,5},{5... | collective-permute-start | bytes 196616 | tf_op jit(solution)/shard_map/ppermute | solution.py:199
  28.0 2.8 %collective-permute-start.12 = (f32[128,128]{1,0:T(8,128)S(1)}, f32[128,128]{1,0:T(8,128)S(1)}, u32[]{:S(2)}, u32[]{:S(2)}) collective-permute-start(f32[128,128]{1,0:T(8,128)S(1)} %get-tuple-element.14), channel_id=1, source_target_pairs={{0,4},{4,0},{8,12},{12,8},{16,20},{20,16},{24,28},{28,24},{1,5},{5... | collective-permute-start | bytes 196616 | tf_op jit(solution)/shard_map/ppermute | solution.py:199
  28.5 2.9 %collective-permute-start.14 = (f32[128,128]{1,0:T(8,128)S(1)}, f32[128,128]{1,0:T(8,128)S(1)}, u32[]{:S(2)}, u32[]{:S(2)}) collective-permute-start(f32[128,128]{1,0:T(8,128)S(1)} %get-tuple-element.16), channel_id=1, source_target_pairs={{0,4},{4,0},{8,12},{12,8},{16,20},{20,16},{24,28},{28,24},{1,5},{5... | collective-permute-start | bytes 196616 | tf_op jit(solution)/shard_map/ppermute | solution.py:199
  28.6 5.0 %collective-permute-start.16 = (f32[128,128]{1,0:T(8,128)S(1)}, f32[128,128]{1,0:T(8,128)S(1)}, u32[]{:S(2)}, u32[]{:S(2)}) collective-permute-start(f32[128,128]{1,0:T(8,128)S(1)} %get-tuple-element.18), channel_id=1, source_target_pairs={{0,4},{4,0},{8,12},{12,8},{16,20},{20,16},{24,28},{28,24},{1,5},{5... | collective-permute-start | bytes 196616 | tf_op jit(solution)/shard_map/ppermute | solution.py:199
  29.2 5.2 %collective-permute-start.11 = (f32[128,128]{1,0:T(8,128)S(1)}, f32[128,128]{1,0:T(8,128)S(1)}, u32[]{:S(2)}, u32[]{:S(2)}) collective-permute-start(f32[128,128]{1,0:T(8,128)S(1)} %add.21), channel_id=1, source_target_pairs={{0,24},{4,28},{8,16},{12,20},{16,8},{20,12},{24,0},{28,4},{1,25},{... | collective-permute-start | bytes 196616 | tf_op jit(solution)/shard_map/ppermute | solution.py:199
  30.8 5.0 %collective-permute-start.13 = (f32[128,128]{1,0:T(8,128)S(1)}, f32[128,128]{1,0:T(8,128)S(1)}, u32[]{:S(2)}, u32[]{:S(2)}) collective-permute-start(f32[128,128]{1,0:T(8,128)S(1)} %add.22), channel_id=1, source_target_pairs={{0,16},{4,20},{8,24},{12,28},{16,0},{20,4},{24,8},{28,12},{1,17},{... | collective-permute-start | bytes 196616 | tf_op jit(solution)/shard_map/ppermute | solution.py:199
  31.4 4.4 %collective-permute-start.15 = (f32[128,128]{1,0:T(8,128)S(1)}, f32[128,128]{1,0:T(8,128)S(1)}, u32[]{:S(2)}, u32[]{:S(2)}) collective-permute-start(f32[128,128]{1,0:T(8,128)S(1)} %add.24), channel_id=1, source_target_pairs={{0,8},{4,12},{8,0},{12,4},{16,24},{20,28},{24,16},{28,20},{1,9},{5... | collective-permute-start | bytes 196616 | tf_op jit(solution)/shard_map/ppermute | solution.py:199
